TPU v7x, 32 devices: a whole 2x2x4 slice. The times are simulated.
32 devices in a mesh: patch: 8 (over z, y), sub: 4 (over x, core).
Axes of the slice: x: 2, y: 2, z: 4, core: 2. Of those that a mesh axis runs over, the one named last changes fastest.
Arguments:
- state: float32 [8, 4, 1, 27, 729], P('patch', 'sub'), may hold values from -6 to 6
- stiff_weight: float32 [8, 96, 9216], P('patch'), may hold values from 0.3 to 3
- volume_weight: float32 [8, 96, 9216], P('patch'), may hold values from 0.5 to 2
- lagrange: float32 [32, 4, 1, 729], P('patch', 'sub'), may hold values from -6 to 6
- mortar: float32 [32, 2, 2, 27, 27], P('patch'), may hold values from -1.25 to 1.25
- links: int32 [32, 6], replicated, may hold values from 0 to 27, as said below
Outputs:
- residual: float32 [8, 4, 1, 27, 729], P('patch', 'sub')
- constraint: float32 [32, 4, 1, 729], P('patch', 'sub')
Inputs may be any that keep to these rules, and one draw needn't show every extreme that they name: `links`: row o * 4 + s is slot s of owner o along patch. Live slots of an owner come first and have both counts in 12 to 27; empty slots are all zero. 2 * 8 slots are live. A live interface joins face 2d + 1 of its first patch to face 2d of its second patch, d being 0 or 1; faces 0 to 3 of every patch lie on exactly one live interface each; the live interfaces of one owner all have the same d. At most 2 faces of one patch lie on live interfaces of one owner; in every draw some owner has 4 live slots and 2 faces of one patch.
All inputs are finite; a program needn't handle non-finite values.
Results may differ from a plain program's by a relative error of at most 0.0001.
Values sent between devices are 32-bit elements; how exact they have to be, the bound alone decides.
No kernel may reach another device: no remote copies, remote signals or barrier semaphores. Data moves between devices by JAX's collectives and lax.ppermute only.
A program may use at most 128 MiB of HBM per device.

v0:
```python
import functools

import jax
import jax.numpy as jnp
import numpy as np
from jax import lax
from jax.experimental import pallas as pl
from jax.experimental.pallas import tpu as pltpu
from jax.sharding import PartitionSpec as P

ELEMS = 24
DEGREE = 3
FIELDS = 4
LOCAL = DEGREE + 1
NODES = 4
BASIS = ELEMS + DEGREE
QUAD = ELEMS * NODES
PAD = 32
WIN = LOCAL * PAD
SPAN = NODES * QUAD
GROUPS = ELEMS // 4
WIDE = (GROUPS + 1) * WIN
FLAT = 768

stabilize = 0.25
highest = lax.Precision.HIGHEST
f32 = jnp.float32
bf16 = jnp.bfloat16
gauss_points_four = [
    -0.8611363115940526,
    -0.3399810435848563,
    0.3399810435848563,
    0.8611363115940526,
]
gauss_weights_four = [
    0.3478548451374538,
    0.6521451548625461,
    0.6521451548625461,
    0.3478548451374538,
]


def spline_tables(knot_list, points, degree):
    current = np.where(
        (knot_list[None, :-1] <= points[:, None]) & (points[:, None] < knot_list[None, 1:]),
        1.0,
        0.0,
    )
    previous = current
    for order_k in range(1, degree + 1):
        previous = current
        amount = len(knot_list) - 1 - order_k
        current = np.zeros((points.shape[0], amount))
        for column in range(amount):
            left_span = knot_list[column + order_k] - knot_list[column]
            right_span = knot_list[column + order_k + 1] - knot_list[column + 1]
            if left_span > 0:
                current[:, column] += (points - knot_list[column]) / left_span * previous[:, column]
            if right_span > 0:
                current[:, column] += (
                    (knot_list[column + order_k + 1] - points)
                    / right_span
                    * previous[:, column + 1]
                )
    slope_part = np.zeros(current.shape)
    for column in range(current.shape[1]):
        left_span = knot_list[column + degree] - knot_list[column]
        right_span = knot_list[column + degree + 1] - knot_list[column + 1]
        if left_span > 0:
            slope_part[:, column] += degree / left_span * previous[:, column]
        if right_span > 0:
            slope_part[:, column] -= degree / right_span * previous[:, column + 1]
    return current, slope_part


def halves(table):
    high = table.astype(np.dtype(bf16)).astype(np.float64)
    return high, table - high


def padded(table, rows, cols):
    out = np.zeros((rows, cols))
    out[: table.shape[0], : table.shape[1]] = table
    return out


@functools.cache
def constants():
    nodes = np.array(gauss_points_four)
    points = (np.arange(ELEMS)[:, None] + (nodes[None, :] + 1.0) / 2.0).reshape(-1)
    weights = np.tile(np.array(gauss_weights_four) / 2.0, ELEMS)
    open_knots = np.concatenate(
        [np.zeros(DEGREE), np.arange(ELEMS + 1.0), np.full(DEGREE, float(ELEMS))]
    )
    even_knots = np.arange(-DEGREE, ELEMS + DEGREE + 1.0)
    value, slope = spline_tables(open_knots, points, DEGREE)
    even_value, even_slope = spline_tables(even_knots, points, DEGREE)
    change = np.round(np.linalg.lstsq(even_value, value, rcond=None)[0] * 4.0) / 4.0
    local_value = even_value[4 * NODES : 5 * NODES, 4 : 4 + LOCAL]
    local_slope = even_slope[4 * NODES : 5 * NODES, 4 : 4 + LOCAL]
    local_w = weights[:NODES, None]

    def kron(local, table):
        wide = padded(table, QUAD, PAD)
        return np.einsum("bj,ck->jkbc", local, wide).reshape(WIN, SPAN)

    ahead = np.concatenate(
        [kron(local_value, value), kron(local_slope, value), kron(local_value, slope)], axis=1
    )
    value_w, slope_w = value * weights[:, None], slope * weights[:, None]
    back = np.concatenate(
        [
            kron(local_value * local_w, value_w).T,
            kron(local_slope * local_w, value_w).T,
            kron(local_value * local_w, slope_w).T,
            ],
        axis=0,
    )
    ahead_high, ahead_low = halves(ahead)
    ahead3 = np.concatenate([ahead_high, ahead_high, ahead_low], axis=0)
    back_high, back_low = halves(back)
    back2 = np.concatenate([back_high, back_low], axis=1)

    def left3(table):
        high, low = halves(padded(table, QUAD, PAD))
        return np.concatenate([high, high, low], axis=1)

    def left4(table):
        high, low = halves(padded(table, QUAD, PAD).T)
        return np.concatenate(
            [np.concatenate([high, high], axis=1), np.concatenate([low, low], axis=1)], axis=0
        )

    spread = np.zeros((BASIS, BASIS, WIDE // PAD, PAD))
    for k in range(BASIS):
        spread[:, k, :BASIS, k] = change.T
    spread = padded(spread.reshape(BASIS * BASIS, WIDE), FLAT, WIDE)
    fold = np.zeros((FLAT, PAD))
    for j in range(BASIS):
        fold[j * BASIS : (j + 1) * BASIS, :BASIS] = np.eye(BASIS)
    group = np.full((8, FLAT), 99, np.int32)
    group[:, : BASIS * BASIS] = np.arange(BASIS * BASIS)[None, :] // BASIS
    as16 = lambda a: a.astype(np.dtype(bf16))
    return dict(
        ahead=as16(ahead3),
        back=as16(back2),
        outer=as16(np.stack([left3(slope), left3(value)])),
        inner=as16(np.stack([left4(slope_w), left4(value_w)])),
        spread=as16(spread),
        fold=as16(fold),
        group=group,
    )


def split(x):
    high = x.astype(bf16)
    return high, (x - high.astype(f32)).astype(bf16)


def dot(a, b):
    return jnp.dot(a, b, preferred_element_type=f32)


def dot_nt(a, b):
    return lax.dot_general(a, b, (((1,), (1,)), ((), ())), preferred_element_type=f32)


def expand(fields, spread):
    count = len(fields)
    parts = []
    for field in fields:
        parts.extend(split(field))
    out = dot(jnp.concatenate(parts, axis=0), spread)
    return [out[2 * n * PAD : (2 * n + 1) * PAD] + out[(2 * n + 1) * PAD : (2 * n + 2) * PAD] for n in range(count)]


def windows(wide, groups):
    shifted = [wide] + [pltpu.roll(wide, WIDE - PAD * r, axis=1) for r in range(1, 4)]
    shifted = [split(x) for x in shifted]
    rows = []
    for m in groups:
        for r in range(4):
            high = shifted[r][0][:, m * WIN : (m + 1) * WIN]
            low = shifted[r][1][:, m * WIN : (m + 1) * WIN]
            rows.append(jnp.concatenate([high, low, high], axis=1))
    return jnp.concatenate(rows, axis=0)


def overlap(rows, groups):
    first, count = groups[0], len(groups)
    total = None
    for r in range(4):
        pieces = []
        if first > 0:
            pieces.append(jnp.zeros((PAD, first * WIN), f32))
        pieces.extend(rows[(4 * n + r) * PAD : (4 * n + r + 1) * PAD] for n in range(count))
        rest = WIDE // WIN - first - count
        pieces.append(jnp.zeros((PAD, rest * WIN), f32))
        line = jnp.concatenate(pieces, axis=1)
        if r > 0:
            line = pltpu.roll(line, PAD * r, axis=1)
        total = line if total is None else total + line
    return total


def gather_back(heads, back, count):
    out = dot(heads, back)
    rows = count * PAD
    out = out[:rows] + out[rows:]
    return out[:, :WIN] + out[:, WIN:]


def load_flat(dst, src):
    dst[...] = jnp.zeros(dst.shape, f32)
    dst[:BASIS, : BASIS * BASIS] = src


def stiff_kernel(groups, expand_here, field_ref, spread_ref, ahead_ref, outer_ref, inner_ref, back_ref, weight_hbm, *rest):
    if expand_here:
        out_ref, wide_ref, flat, weight, mid_h, mid_l, heads, sems = rest
    else:
        out_ref, weight, mid_h, mid_l, heads, sems = rest
    step = 4 * SPAN
    copies = [
        pltpu.make_async_copy(
            weight_hbm.at[0, :, pl.ds(m * step, step)], weight.at[:, pl.ds(n * step, step)], sems.at[n]
        )
        for n, m in enumerate(groups)
    ]
    for copy in copies:
        copy.start()
    if expand_here:
        load_flat(flat, field_ref[0, 0, 0])
        (wide,) = expand([flat[...]], spread_ref[...])
        wide_ref[...] = wide
    else:
        wide = field_ref[...]
    lhs = windows(wide, groups)
    count = 4 * len(groups)
    rows = count * PAD
    mid = dot(lhs, ahead_ref[...])
    high, low = split(mid)
    mid_h[...] = high
    mid_l[...] = low
    for n in range(len(groups)):
        copies[n].wait()
        for r in range(4):
            e = 4 * n + r
            at = slice(e * PAD, (e + 1) * PAD)
            stack = jnp.concatenate([mid_h[at, :], mid_l[at, :], mid_h[at, :]], axis=0)
            first = dot(outer_ref[0], stack[:, :SPAN])
            others = dot(outer_ref[1], stack[:, SPAN:])
            scale = weight[:, e * SPAN : (e + 1) * SPAN]
            first = first * scale
            others = others * jnp.concatenate([scale, scale], axis=1)
            first = dot(inner_ref[0], jnp.concatenate(split(first), axis=0))
            others = dot(inner_ref[1], jnp.concatenate(split(others), axis=0))
            high, low = split(first[:PAD] + first[PAD:])
            heads[at, :SPAN] = high
            heads[rows + e * PAD : rows + (e + 1) * PAD, :SPAN] = low
            high, low = split(others[:PAD] + others[PAD:])
            heads[at, SPAN:] = high
            heads[rows + e * PAD : rows + (e + 1) * PAD, SPAN:] = low
    out_ref[...] = overlap(gather_back(heads[...], back_ref[...], count), groups)


def volume_kernel(place_ref, near_ref, far_ref, spread_ref, ahead_ref, outer_ref, inner_ref, back_ref, weight_hbm, out_ref, flat, weight, mid_h, mid_l, heads, sems):
    groups = list(range(GROUPS))
    step = 4 * SPAN
    copies = [
        pltpu.make_async_copy(
            weight_hbm.at[0, :, pl.ds(m * step, step)], weight.at[:, pl.ds(m * step, step)], sems.at[m]
        )
        for m in groups
    ]
    for copy in copies:
        copy.start()
    sub = place_ref[1]
    is_pressure = sub == FIELDS - 1
    load_flat(flat.at[0], near_ref[0, 0, 0])
    load_flat(flat.at[1], far_ref[0])
    load_flat(flat.at[2], far_ref[1])
    chosen = jnp.where(is_pressure, 2, 2 - sub)
    zero = jnp.zeros((PAD, FLAT), f32)
    fields = [
        flat[chosen],
        jnp.where(is_pressure, flat[1], zero),
        jnp.where(is_pressure, flat[0], zero),
    ]
    wides = expand(fields, spread_ref[...])
    count = 4 * len(groups)
    rows = count * PAD
    mid = dot(windows(wides[0], groups), ahead_ref[:, :SPAN])
    high, low = split(mid)
    mid_h[:, :SPAN] = high
    mid_l[:, :SPAN] = low
    mid = dot(windows(wides[1], groups), ahead_ref[:, SPAN : 2 * SPAN]) + dot(
        windows(wides[2], groups), ahead_ref[:, 2 * SPAN :]
    )
    high, low = split(mid)
    mid_h[:, SPAN:] = high
    mid_l[:, SPAN:] = low
    along = jnp.where(is_pressure, 0, 1)
    outer = jnp.concatenate([outer_ref[along], outer_ref[1]], axis=1)
    inner = inner_ref[jnp.where(sub == 0, 0, 1)]
    for n in range(len(groups)):
        copies[n].wait()
        for r in range(4):
            e = 4 * n + r
            at = slice(e * PAD, (e + 1) * PAD)
            stack = jnp.concatenate(
                [mid_h[at, :SPAN], mid_l[at, :SPAN], mid_h[at, :SPAN], mid_h[at, SPAN:], mid_l[at, SPAN:], mid_h[at, SPAN:]],
                axis=0,
            )
            value = dot(outer, stack) * weight[:, e * SPAN : (e + 1) * SPAN]
            value = dot(inner, jnp.concatenate(split(value), axis=0))
            high, low = split(value[:PAD] + value[PAD:])
            heads[at, :] = high
            heads[rows + e * PAD : rows + (e + 1) * PAD, :] = low
    kind = jnp.where(is_pressure, 0, sub)
    back = back_ref[pl.ds(pl.multiple_of(kind * SPAN, SPAN), SPAN), :]
    out_ref[...] = overlap(gather_back(heads[...], back, count), groups)


def masked(matrix, limit):
    rows = lax.broadcasted_iota(jnp.int32, matrix.shape, 0)
    return jnp.where(rows < limit, matrix, 0.0)


def prep_kernel(links_ref, place_ref, field_ref, lag_ref, mortar_ref, fold_ref, group_ref, out_ref, flat, line):
    slots = lag_ref.shape[0]
    out_ref[...] = jnp.zeros(out_ref.shape, f32)
    load_flat(flat, field_ref[0, 0, 0])
    line[...] = jnp.zeros(line.shape, f32)
    for s in range(slots):
        line[s : s + 1, : BASIS * BASIS] = lag_ref[s, 0]
    lanes = jnp.broadcast_to(group_ref[0:1, :], (PAD, FLAT))
    rows = lax.broadcasted_iota(jnp.int32, (PAD, FLAT), 0)
    same = rows == lanes
    spreads = [
        jnp.where(same, flat[0:1, :], 0.0),
        jnp.where(same, flat[BASIS - 1 : BASIS, :], 0.0),
        jnp.where(lanes == 0, flat[...], 0.0),
        jnp.where(lanes == BASIS - 1, flat[...], 0.0),
    ]
    for s in range(slots):
        spreads.append(jnp.where(same, line[s : s + 1, :], 0.0))
    parts = []
    for x in spreads:
        parts.extend(split(x))
    out = dot(jnp.concatenate(parts, axis=0), fold_ref[...])
    squares = [out[2 * n * PAD : (2 * n + 1) * PAD] + out[(2 * n + 1) * PAD : (2 * n + 2) * PAD] for n in range(4 + slots)]
    for f in range(4):
        out_ref[0, :, f * PAD : (f + 1) * PAD] = squares[f]
    base = place_ref[0] * slots
    for s in range(slots):
        limits = (links_ref[base + s, 4], links_ref[base + s, 5])
        multiplier = squares[4 + s][:BASIS, :BASIS]
        for side in range(2):
            left = masked(mortar_ref[s, side, 0], limits[0])
            right = masked(mortar_ref[s, side, 1], limits[1])
            half = lax.dot_general(
                left, multiplier, (((0,), (0,)), ((), ())), precision=highest, preferred_element_type=f32
            )
            both = jnp.dot(half, right, precision=highest, preferred_element_type=f32)
            item = 2 * s + side
            at = (item % 4) * PAD
            out_ref[1 + item // 4, :BASIS, at : at + BASIS] = both if side == 0 else -both


def position(mine, other, masks):
    differ = jnp.bitwise_xor(mine, other)
    total = jnp.int32(0)
    for n, mask in enumerate(masks):
        total = total + jnp.where(jnp.bitwise_and(differ, mask) != 0, jnp.int32(1 << n), jnp.int32(0))
    return total


def final_kernel(masks, links_ref, place_ref, *refs):
    rounds = len(masks)
    part_refs = refs[: rounds + 1]
    stiff_a, stiff_b, volume_ref, spread_ref, fold_ref, group_ref, mortar_ref, out_ref, jump_ref, buf, found = refs[rounds + 1 :]
    slots = mortar_ref.shape[0]
    mine = place_ref[0]
    table = links_ref.shape[0]
    buf[0] = part_refs[0][...]
    for n in range(rounds):
        buf[(1 << n) : (2 << n)] = part_refs[n + 1][...].reshape((1 << n,) + buf.shape[1:])
    for f in range(8):
        found[f] = 0

    def look(t, carry):
        for side in range(2):
            hit = jnp.logical_and(links_ref[t, side] == mine, links_ref[t, 4] > 0)
            where = jnp.where(hit, links_ref[t, 2 + side], 4)
            found[where] = 2 * t + side
        return carry

    lax.fori_loop(0, table, look, 0, unroll=8)

    def pick(owner, plane, lane):
        block = buf[position(mine, owner, masks), plane]
        return pltpu.roll(block, lax.rem(WIN - lane * PAD, WIN), axis=1)[:, :PAD]

    squares = []
    for f in range(4):
        item = found[f]
        owner = lax.div(item, 2 * slots)
        item = lax.rem(item, 2 * slots)
        squares.append(pick(owner, 1 + lax.div(item, 4), lax.rem(item, 4)))
    base = mine * slots
    for s in range(slots):
        limits = (links_ref[base + s, 4], links_ref[base + s, 5])
        total = None
        for side in range(2):
            trace = pick(links_ref[base + s, side], 0, links_ref[base + s, 2 + side])
            trace = trace[:BASIS, :BASIS]
            left = masked(mortar_ref[s, side, 0], limits[0])
            right = masked(mortar_ref[s, side, 1], limits[1])
            half = jnp.dot(left, trace, precision=highest, preferred_element_type=f32)
            both = lax.dot_general(
                half, right, (((1,), (1,)), ((), ())), precision=highest, preferred_element_type=f32
            )
            total = both if total is None else total - both
        squares.append(jnp.pad(total, ((0, PAD - BASIS), (0, PAD - BASIS))))
    parts = []
    for x in squares:
        parts.extend(split(x))
    flat = dot_nt(jnp.concatenate(parts, axis=0), fold_ref[...])
    lines = [flat[2 * n * PAD : (2 * n + 1) * PAD] + flat[(2 * n + 1) * PAD : (2 * n + 2) * PAD] for n in range(4 + slots)]
    lanes = jnp.broadcast_to(group_ref[0:1, :], (PAD, FLAT))
    rows = lax.broadcasted_iota(jnp.int32, (PAD, FLAT), 0)
    same = rows == lanes
    for s in range(slots):
        row = jnp.sum(jnp.where(same, lines[4 + s], 0.0), axis=0, keepdims=True)
        jump_ref[s, 0] = row[:, : BASIS * BASIS]
    is_pressure = place_ref[1] == FIELDS - 1
    factor = jnp.where(is_pressure, -stabilize, 1.0).astype(f32)
    total = factor * (stiff_a[...] + stiff_b[...]) - volume_ref[...]
    out = dot_nt(jnp.concatenate(split(total), axis=0), spread_ref[...])
    out = out[:PAD] + out[PAD:]
    low_row = jnp.sum(jnp.where(same, lines[0], 0.0), axis=0, keepdims=True)
    high_row = jnp.sum(jnp.where(same, lines[1], 0.0), axis=0, keepdims=True)
    out = out + jnp.where(rows == 0, low_row, 0.0) + jnp.where(rows == BASIS - 1, high_row, 0.0)
    out = out + jnp.where(lanes == 0, lines[2], 0.0) + jnp.where(lanes == BASIS - 1, lines[3], 0.0)
    out_ref[0, 0, 0] = out[:BASIS, : BASIS * BASIS]


def vmem():
    return pl.BlockSpec(memory_space=pltpu.VMEM)


def smem():
    return pl.BlockSpec(memory_space=pltpu.SMEM)


def anywhere():
    return pl.BlockSpec(memory_space=pl.ANY)


params = pltpu.CompilerParams(vmem_limit_bytes=48 << 20)


def stiff_call(groups, expand_here, field, tables, weight):
    count = 4 * len(groups)
    scratch = [
        pltpu.VMEM((QUAD, count * SPAN), f32),
        pltpu.VMEM((count * PAD, 3 * SPAN), bf16),
        pltpu.VMEM((count * PAD, 3 * SPAN), bf16),
        pltpu.VMEM((2 * count * PAD, 3 * SPAN), bf16),
        pltpu.SemaphoreType.DMA((len(groups),)),
    ]
    wide = jax.ShapeDtypeStruct((PAD, WIDE), f32)
    if expand_here:
        scratch = [pltpu.VMEM((PAD, FLAT), f32)] + scratch
    return pl.pallas_call(
        functools.partial(stiff_kernel, groups, expand_here),
        out_shape=(wide, wide) if expand_here else wide,
        in_specs=[vmem()] * 6 + [anywhere()],
        out_specs=(vmem(), vmem()) if expand_here else vmem(),
        scratch_shapes=scratch,
        compiler_params=params,
    )(field, tables["spread"], tables["ahead"], tables["outer"], tables["inner"], tables["back"], weight)


def volume_call(place, near, far, tables, weight):
    return pl.pallas_call(
        volume_kernel,
        out_shape=jax.ShapeDtypeStruct((PAD, WIDE), f32),
        in_specs=[smem()] + [vmem()] * 7 + [anywhere()],
        out_specs=vmem(),
        scratch_shapes=[
            pltpu.VMEM((3, PAD, FLAT), f32),
            pltpu.VMEM((QUAD, ELEMS * SPAN), f32),
            pltpu.VMEM((ELEMS * PAD, 2 * SPAN), bf16),
            pltpu.VMEM((ELEMS * PAD, 2 * SPAN), bf16),
            pltpu.VMEM((2 * ELEMS * PAD, SPAN), bf16),
            pltpu.SemaphoreType.DMA((GROUPS,)),
        ],
        compiler_params=params,
    )(place, near, far, tables["spread"], tables["ahead"], tables["outer"], tables["inner"], tables["back"], weight)


def swap(array, axis, mask):
    size = lax.axis_size(axis)
    return lax.ppermute(array, axis, [(n, n ^ mask) for n in range(size)])


def per_device(state, stiff_weight, volume_weight, lagrange, mortar, links):
    tables = {name: jnp.asarray(value) for name, value in constants().items()}
    patches = lax.axis_size("patch")
    place = jnp.stack([lax.axis_index("patch"), lax.axis_index("sub")]).astype(jnp.int32)
    slots = mortar.shape[0]
    planes = 1 + (2 * slots + 3) // 4
    masks = [1 << n for n in reversed(range(patches.bit_length() - 1))]

    near = swap(state, "sub", 1)
    far = swap(jnp.concatenate([state[0, 0], near[0, 0]], axis=0), "sub", 2)
    own = pl.pallas_call(
        prep_kernel,
        out_shape=jax.ShapeDtypeStruct((planes, PAD, WIN), f32),
        in_specs=[smem(), smem()] + [vmem()] * 5,
        out_specs=vmem(),
        scratch_shapes=[pltpu.VMEM((PAD, FLAT), f32), pltpu.VMEM((8, FLAT), f32)],
        compiler_params=params,
    )(links, place, state, lagrange, mortar, tables["fold"], tables["group"])
    parts = [own]
    held = own
    for mask in masks:
        other = swap(held, "patch", mask)
        parts.append(other)
        held = jnp.concatenate([held, other], axis=0)

    half = GROUPS // 2
    stiff_a, wide = stiff_call(list(range(half)), True, state, tables, stiff_weight)
    stiff_b = stiff_call(list(range(half, GROUPS)), False, wide, tables, stiff_weight)
    volume = volume_call(place, near, far, tables, volume_weight)
    return pl.pallas_call(
        functools.partial(final_kernel, masks),
        out_shape=(
            jax.ShapeDtypeStruct(state.shape, f32),
            jax.ShapeDtypeStruct((slots, 1, 1, BASIS * BASIS), f32),
        ),
        in_specs=[smem(), smem()] + [vmem()] * (len(parts) + 7),
        out_specs=(vmem(), vmem()),
        scratch_shapes=[pltpu.VMEM((patches, planes, PAD, WIN), f32), pltpu.SMEM((8,), jnp.int32)],
        compiler_params=params,
    )(links, place, *parts, stiff_a, stiff_b, volume, tables["spread"], tables["fold"], tables["group"], mortar)


def solution(mesh):
    return jax.shard_map(
        per_device,
        mesh=mesh,
        in_specs=(
            P("patch", "sub", None, None, None),
            P("patch", None, None),
            P("patch", None, None),
            P("patch", "sub", None, None),
            P("patch", None, None, None, None),
            P(),
        ),
        out_specs=(P("patch", "sub", None, None, None), P("patch", "sub", None, None)),
        check_vma=False,
    )
```

profile of v0, /device:TPU:0, one launch (start us, length us, event | category | flops | bytes accessed | tf_op | source)
XLA Modules:
  0.0 52.3 jit_solution(11619993444372037241)
XLA Ops:
  0.6 0.8 %copy.29.links_ref = s32[32,6]{1,0:T(8,128)S(1)} copy(s32[32,6]{0,1:T(8,128)} %param.18) | data formatting | bytes 1536 | tf_op args[5]
  1.4 0.9 %copy.24.field_ref = f32[1,1,1,27,729]{4,3,2,1,0:T(8,128)S(1)} copy(f32[1,1,1,27,729]{4,2,3,1,0:T(1,128)} %param.13) | data formatting | bytes 157464 | tf_op args[0]
  2.3 1.0 %copy.25.mortar_ref.refs_10_ = f32[4,2,2,27,27]{4,3,2,1,0:T(8,128)S(1)} copy(f32[4,2,2,27,27]{4,2,3,1,0:T(2,128)} %param.17) | data formatting | bytes 93312 | tf_op args[4]
  3.3 0.1 pad_add_fusion.place_ref
  3.3 0.9 %copy-done.6 = bf16[768,32]{1,0:T(8,128)(2,1)S(1)} copy-done((bf16[768,32]{1,0:T(8,128)(2,1)S(1)}, bf16[768,32]{1,0:T(8,128)(2,1)}, u32[]{:S(2)}) %copy-start.6) | copy-done | bytes 49176
  4.3 0.7 %copy-done.10 = s32[8,768]{1,0:T(8,128)S(1)} copy-done((s32[8,768]{1,0:T(8,128)S(1)}, s32[8,768]{1,0:T(8,128)}, u32[]{:S(2)}) %copy-start.10) | copy-done | bytes 24600
  5.0 0.7 %copy-done.11 = f32[4,1,1,729]{3,2,1,0:T(1,128)S(1)} copy-done((f32[4,1,1,729]{3,2,1,0:T(1,128)S(1)}, f32[4,1,1,729]{3,2,1,0:T(1,128)}, u32[]{:S(2)}) %copy-start.11) | copy-done | bytes 11688
  5.7 3.1 %shard_map.140.refs_0_ = f32[3,32,128]{2,1,0:T(8,128)S(1)} custom-call(s32[32,6]{1,0:T(8,128)S(1)} %copy.29.links_ref, s32[2]{0:T(128)S(1)} %pad_add_fusion.place_ref, f32[1,1,1,27,729]{4,3,2,1,0:T(8,128)S(1)} %copy.24.field_ref, f32[4,1,1,729]{3,2,1,0:T(1,128)S(1)} %copy-done.11, f32[4,2,2,27,27]{4,3,2,1,0:T(8,128)S(1)} %copy.25.mortar_ref.refs_10_, ...), custom_call_target="tpu_custom_call" | custom-call | tf_op jit(solution)/shard_map/pallas_call | solution.py:519
  8.8 4.1 %collective-permute-start = (f32[3,32,128]{2,1,0:T(8,128)S(1)}, f32[3,32,128]{2,1,0:T(8,128)S(1)}, u32[]{:S(2)}, u32[]{:S(2)}) collective-permute-start(f32[3,32,128]{2,1,0:T(8,128)S(1)} %shard_map.140.refs_0_), channel_id=1, source_target_pairs={{0,16},{4,20},{8,24},{12,28},{16,0},{20,4},{24,8},{28,12},{1,17},{... | collective-permute-start | bytes 147464 | tf_op jit(solution)/shard_map/ppermute | solution.py:506
  12.9 2.6 %collective-permute-done.refs_1_ = f32[3,32,128]{2,1,0:T(8,128)S(1)} collective-permute-done((f32[3,32,128]{2,1,0:T(8,128)S(1)}, f32[3,32,128]{2,1,0:T(8,128)S(1)}, u32[]{:S(2)}, u32[]{:S(2)}) %collective-permute-start) | collective-permute-done | bytes 49184 | tf_op jit(solution)/shard_map/ppermute | solution.py:506
  15.5 1.4 %collective-permute-start.1 = (f32[6,32,128]{2,1,0:T(8,128)S(1)}, f32[6,32,128]{2,1,0:T(8,128)S(1)}, u32[]{:S(2)}, u32[]{:S(2)}) collective-permute-start(f32[6,32,128]{2,1,0:T(8,128)S(1)} %pad_maximum_fusion.2), channel_id=1, source_target_pairs={{0,8},{4,12},{8,0},{12,4},{16,24},{20,28},{24,16},{28,20},{1,9},{5... | collective-permute-start | bytes 294920 | tf_op jit(solution)/shard_map/ppermute | solution.py:506
  16.9 0.0 collective-permute-start.3
  16.9 1.0 %copy.28 = f32[1,27,729]{2,1,0:T(8,128)S(1)} copy(f32[1,27,729]{2,0,1:T(1,128)} %bitcast.5) | data formatting | bytes 157464 | tf_op jit(solution)/shard_map/squeeze | solution.py:518
  17.9 2.3 %collective-permute-done.1.refs_2_ = f32[6,32,128]{2,1,0:T(8,128)S(1)} collective-permute-done((f32[6,32,128]{2,1,0:T(8,128)S(1)}, f32[6,32,128]{2,1,0:T(8,128)S(1)}, u32[]{:S(2)}, u32[]{:S(2)}) %collective-permute-start.1) | collective-permute-done | bytes 98336 | tf_op jit(solution)/shard_map/ppermute | solution.py:506
  20.2 1.8 %collective-permute-start.2 = (f32[12,32,128]{2,1,0:T(8,128)S(1)}, f32[12,32,128]{2,1,0:T(8,128)S(1)}, u32[]{:S(2)}, u32[]{:S(2)}) collective-permute-start(f32[12,32,128]{2,1,0:T(8,128)S(1)} %pad_maximum_fusion), channel_id=1, source_target_pairs={{0,4},{4,0},{8,12},{12,8},{16,20},{20,16},{24,28},{28,24},{1,5},{5... | collective-permute-start | bytes 589832 | tf_op jit(solution)/shard_map/ppermute | solution.py:506
  22.0 0.0 collective-permute-done.3.near_ref
  22.0 1.6 %collective-permute-start.4 = (f32[2,27,729]{2,1,0:T(8,128)S(1)}, f32[2,27,729]{2,1,0:T(8,128)S(1)}, u32[]{:S(2)}, u32[]{:S(2)}) collective-permute-start(f32[2,27,729]{2,1,0:T(8,128)S(1)} %pad_maximum_fusion.1), channel_id=1, source_target_pairs={{0,2},{1,3},{2,0},{3,1},{4,6},{5,7},{6,4},{7,5},{8,10},{9,11},{10,... | collective-permute-start | bytes 472400 | tf_op jit(solution)/shard_map/ppermute | solution.py:506
  23.6 1.3 %copy-done = bf16[768,896]{1,0:T(8,128)(2,1)S(1)} copy-done((bf16[768,896]{1,0:T(8,128)(2,1)S(1)}, bf16[768,896]{1,0:T(8,128)(2,1)}, u32[]{:S(2)}) %copy-start) | copy-done | bytes 1376280
  24.9 1.2 %copy-done.2 = bf16[384,1152]{1,0:T(8,128)(2,1)S(1)} copy-done((bf16[384,1152]{1,0:T(8,128)(2,1)S(1)}, bf16[384,1152]{1,0:T(8,128)(2,1)}, u32[]{:S(2)}) %copy-start.2) | copy-done | bytes 884760
  26.1 1.1 %copy-done.4 = bf16[1152,256]{1,0:T(8,128)(2,1)S(1)} copy-done((bf16[1152,256]{1,0:T(8,128)(2,1)S(1)}, bf16[1152,256]{1,0:T(8,128)(2,1)}, u32[]{:S(2)}) %copy-start.4) | copy-done | bytes 589848
  27.1 0.8 %copy-done.8 = bf16[2,64,192]{2,1,0:T(8,128)(2,1)S(1)} copy-done((bf16[2,64,192]{2,1,0:T(8,128)(2,1)S(1)}, bf16[2,64,192]{2,1,0:T(8,128)(2,1)}, u32[]{:S(2)}) %copy-start.8) | copy-done | bytes 49176
  28.0 0.8 %copy-done.9 = bf16[2,96,96]{2,1,0:T(8,128)(2,1)S(1)} copy-done((bf16[2,96,96]{2,1,0:T(8,128)(2,1)S(1)}, bf16[2,96,96]{2,1,0:T(8,128)(2,1)}, u32[]{:S(2)}) %copy-start.9) | copy-done | bytes 36888
  28.8 5.8 %shard_map.141 = (f32[32,896]{1,0:T(8,128)S(1)}, f32[32,896]{1,0:T(8,128)S(1)}) custom-call(f32[1,1,1,27,729]{4,3,2,1,0:T(8,128)S(1)} %copy.24.field_ref, bf16[768,896]{1,0:T(8,128)(2,1)S(1)} %copy-done, bf16[384,1152]{1,0:T(8,128)(2,1)S(1)} %copy-done.2, bf16[2,96,96]{2,1,0:T(8,128)(2,1)S(1)} %copy-done.9, bf16[2,64,192]{2,1,0:T(8,128)(2,1)S(1)} %copy-done.8, ...), custom_call_target="tpu_custom_call" | custom-call | tf_op jit(solution)/shard_map/pallas_call | solution.py:476
  34.5 0.0 copy-done.3
  34.6 5.5 %shard_map.142.refs_5_ = f32[32,896]{1,0:T(8,128)S(1)} custom-call(f32[32,896]{1,0:T(8,128)S(1)} %get-tuple-element.5.field_ref, bf16[768,896]{1,0:T(8,128)(2,1)S(1)} %copy-done.1, bf16[384,1152]{1,0:T(8,128)(2,1)S(1)} %copy-done.3, bf16[2,96,96]{2,1,0:T(8,128)(2,1)S(1)} %copy-done.9, bf16[2,64,192]{2,1,0:T(8,128)(2,1)S(1)} %copy-done.8, ...), custom_call_target="tpu_custom_call" | custom-call | tf_op jit(solution)/shard_map/pallas_call | solution.py:476
  40.1 0.0 copy-start.7
  40.1 0.0 collective-permute-done.4.far_ref
  40.1 8.3 %shard_map.143.refs_6_ = f32[32,896]{1,0:T(8,128)S(1)} custom-call(s32[2]{0:T(128)S(1)} %pad_add_fusion.place_ref, f32[1,1,1,27,729]{4,3,2,1,0:T(8,128)S(1)} %collective-permute-done.3.near_ref, f32[2,27,729]{2,1,0:T(8,128)S(1)} %collective-permute-done.4.far_ref, bf16[768,896]{1,0:T(8,128)(2,1)S(1)} %copy-done.1, bf16[384,1152]{1,0:T(8,128)(2,1)S(1)} %copy-done.3, ...), custom_call_target="tpu_custom_call" | custom-call | tf_op jit(solution)/shard_map/pallas_call | solution.py:487
  48.4 0.0 collective-permute-done.2.refs_3_
  48.5 0.0 copy-done.7
  48.5 3.2 %shard_map.144 = (f32[1,1,1,27,729]{4,3,2,1,0:T(8,128)S(1)}, f32[4,1,1,729]{3,2,1,0:T(1,128)}) custom-call(s32[32,6]{1,0:T(8,128)S(1)} %copy.29.links_ref, s32[2]{0:T(128)S(1)} %pad_add_fusion.place_ref, f32[3,32,128]{2,1,0:T(8,128)S(1)} %shard_map.140.refs_0_, f32[3,32,128]{2,1,0:T(8,128)S(1)} %collective-permute-done.refs_1_, ...), custom_call_target="tpu_custom_call" | custom-call | tf_op jit(solution)/shard_map/pallas_call | solution.py:538
  51.6 0.7 %copy.31 = f32[1,1,1,27,729]{4,2,3,1,0:T(1,128)} copy(f32[1,1,1,27,729]{4,3,2,1,0:T(8,128)S(1)} %get-tuple-element.8) | data formatting | bytes 157464 | tf_op jit(solution)/shard_map/pallas_call | solution.py:538
  (16 shorter events, 0.1 us)
Async XLA Ops:
  3.3 0.9 %copy-start.6 = (bf16[768,32]{1,0:T(8,128)(2,1)S(1)}, bf16[768,32]{1,0:T(8,128)(2,1)}, u32[]{:S(2)}) copy-start(bf16[768,32]{1,0:T(8,128)(2,1)} %constant.28.clone.fold_ref.refs_8_) | copy-start | bytes 147460
  4.3 0.7 %copy-start.10 = (s32[8,768]{1,0:T(8,128)S(1)}, s32[8,768]{1,0:T(8,128)}, u32[]{:S(2)}) copy-start(s32[8,768]{1,0:T(8,128)} %constant.29.clone.group_ref.refs_9_) | copy-start | bytes 73732
  5.0 0.7 %copy-start.11 = (f32[4,1,1,729]{3,2,1,0:T(1,128)S(1)}, f32[4,1,1,729]{3,2,1,0:T(1,128)}, u32[]{:S(2)}) copy-start(f32[4,1,1,729]{3,2,1,0:T(1,128)} %lag_ref.1) | copy-start | bytes 34996
  8.8 6.7 %collective-permute-start = (f32[3,32,128]{2,1,0:T(8,128)S(1)}, f32[3,32,128]{2,1,0:T(8,128)S(1)}, u32[]{:S(2)}, u32[]{:S(2)}) collective-permute-start(f32[3,32,128]{2,1,0:T(8,128)S(1)} %shard_map.140.refs_0_), channel_id=1, source_target_pairs={{0,16},{4,20},{8,24},{12,28},{16,0},{20,4},{24,8},{28,12},{1,17},{... | collective-permute-start | bytes 147464 | tf_op jit(solution)/shard_map/ppermute | solution.py:506
  15.5 4.7 %collective-permute-start.1 = (f32[6,32,128]{2,1,0:T(8,128)S(1)}, f32[6,32,128]{2,1,0:T(8,128)S(1)}, u32[]{:S(2)}, u32[]{:S(2)}) collective-permute-start(f32[6,32,128]{2,1,0:T(8,128)S(1)} %pad_maximum_fusion.2), channel_id=1, source_target_pairs={{0,8},{4,12},{8,0},{12,4},{16,24},{20,28},{24,16},{28,20},{1,9},{5... | collective-permute-start | bytes 294920 | tf_op jit(solution)/shard_map/ppermute | solution.py:506
  16.9 5.0 %collective-permute-start.3 = (f32[1,1,1,27,729]{4,3,2,1,0:T(8,128)S(1)}, f32[1,1,1,27,729]{4,3,2,1,0:T(8,128)S(1)}, u32[]{:S(2)}, u32[]{:S(2)}) collective-permute-start(f32[1,1,1,27,729]{4,3,2,1,0:T(8,128)S(1)} %copy.24.field_ref), channel_id=1, source_target_pairs={{0,1},{1,0},{2,3},{3,2},{4,5},{5,4},{6,7},{7,6},{8,9},{9,8},{10,11... | collective-permute-start | bytes 236204 | tf_op jit(solution)/shard_map/ppermute | solution.py:506
  16.9 17.6 %copy-start.3 = (bf16[384,1152]{1,0:T(8,128)(2,1)S(1)}, bf16[384,1152]{1,0:T(8,128)(2,1)}, u32[]{:S(2)}) copy-start(bf16[384,1152]{1,0:T(8,128)(2,1)} %constant.23.clone.ahead_ref) | copy-start | bytes 2654212
  20.2 28.3 %collective-permute-start.2 = (f32[12,32,128]{2,1,0:T(8,128)S(1)}, f32[12,32,128]{2,1,0:T(8,128)S(1)}, u32[]{:S(2)}, u32[]{:S(2)}) collective-permute-start(f32[12,32,128]{2,1,0:T(8,128)S(1)} %pad_maximum_fusion), channel_id=1, source_target_pairs={{0,4},{4,0},{8,12},{12,8},{16,20},{20,16},{24,28},{28,24},{1,5},{5... | collective-permute-start | bytes 589832 | tf_op jit(solution)/shard_map/ppermute | solution.py:506
  22.0 18.1 %collective-permute-start.4 = (f32[2,27,729]{2,1,0:T(8,128)S(1)}, f32[2,27,729]{2,1,0:T(8,128)S(1)}, u32[]{:S(2)}, u32[]{:S(2)}) collective-permute-start(f32[2,27,729]{2,1,0:T(8,128)S(1)} %pad_maximum_fusion.1), channel_id=1, source_target_pairs={{0,2},{1,3},{2,0},{3,1},{4,6},{5,7},{6,4},{7,5},{8,10},{9,11},{10,... | collective-permute-start | bytes 472400 | tf_op jit(solution)/shard_map/ppermute | solution.py:506
  23.5 1.3 %copy-start = (bf16[768,896]{1,0:T(8,128)(2,1)S(1)}, bf16[768,896]{1,0:T(8,128)(2,1)}, u32[]{:S(2)}) copy-start(bf16[768,896]{1,0:T(8,128)(2,1)} %constant.27.clone.spread_ref.refs_7_) | copy-start | bytes 4128772
  24.9 1.2 %copy-start.2 = (bf16[384,1152]{1,0:T(8,128)(2,1)S(1)}, bf16[384,1152]{1,0:T(8,128)(2,1)}, u32[]{:S(2)}) copy-start(bf16[384,1152]{1,0:T(8,128)(2,1)} %constant.23.clone.ahead_ref) | copy-start | bytes 2654212
  26.1 1.1 %copy-start.4 = (bf16[1152,256]{1,0:T(8,128)(2,1)S(1)}, bf16[1152,256]{1,0:T(8,128)(2,1)}, u32[]{:S(2)}) copy-start(bf16[1152,256]{1,0:T(8,128)(2,1)} %constant.24.clone.back_ref) | copy-start | bytes 1769476
  27.1 0.8 %copy-start.8 = (bf16[2,64,192]{2,1,0:T(8,128)(2,1)S(1)}, bf16[2,64,192]{2,1,0:T(8,128)(2,1)}, u32[]{:S(2)}) copy-start(bf16[2,64,192]{2,1,0:T(8,128)(2,1)} %constant.26.clone.inner_ref) | copy-start | bytes 147460
  28.0 0.8 %copy-start.9 = (bf16[2,96,96]{2,1,0:T(8,128)(2,1)S(1)}, bf16[2,96,96]{2,1,0:T(8,128)(2,1)}, u32[]{:S(2)}) copy-start(bf16[2,96,96]{2,1,0:T(8,128)(2,1)} %constant.25.clone.outer_ref) | copy-start | bytes 110596
  28.8 5.8 %copy-start.1 = (bf16[768,896]{1,0:T(8,128)(2,1)S(1)}, bf16[768,896]{1,0:T(8,128)(2,1)}, u32[]{:S(2)}) copy-start(bf16[768,896]{1,0:T(8,128)(2,1)} %constant.27.clone.spread_ref.refs_7_) | copy-start | bytes 4128772
  28.8 5.8 %copy-start.5 = (bf16[1152,256]{1,0:T(8,128)(2,1)S(1)}, bf16[1152,256]{1,0:T(8,128)(2,1)}, u32[]{:S(2)}) copy-start(bf16[1152,256]{1,0:T(8,128)(2,1)} %constant.24.clone.back_ref) | copy-start | bytes 1769476
  40.1 8.4 %copy-start.7 = (bf16[768,32]{1,0:T(8,128)(2,1)S(1)}, bf16[768,32]{1,0:T(8,128)(2,1)}, u32[]{:S(2)}) copy-start(bf16[768,32]{1,0:T(8,128)(2,1)} %constant.28.clone.fold_ref.refs_8_) | copy-start | bytes 147460
where the time goes:
time: 53 us; the launch traced here: 52.3 us
  Pallas kernels  25.8 us (49%)
  local copies, waits for them, and re-layouts  11.9 us (22%)
  starting transfers between devices  8.88 us (17%)
  waiting for transfers between devices  4.86 us (9%)
  between operations  0.75 us (1%)
    pallas_call x2, Pallas kernels, stiff_call(): pl.pallas_call(functools.partial(stiff_kernel, groups, expand_here), out_...  11.3 us
    unnamed x27, local copies, waits for them, and re-layouts  10.2 us
    ppermute x5, starting transfers between devices, swap(): return lax.ppermute(array, axis, [(n, n ^ mask) for n in range(size)])  8.88 us
    pallas_call x1, Pallas kernels, volume_call(): pl.pallas_call(volume_kernel, out_shape=jax.ShapeDtypeStruct((PAD, WIDE),...  8.33 us
    ppermute x5, waiting for transfers between devices, swap(): return lax.ppermute(array, axis, [(n, n ^ mask) for n in range(size)])  4.86 us
    pallas_call x1, Pallas kernels, per_device(): pl.pallas_call(functools.partial(final_kernel, masks), out_shape=(jax.Sha...  3.15 us
    pallas_call x1, Pallas kernels, per_device(): pl.pallas_call(prep_kernel, out_shape=jax.ShapeDtypeStruct((planes, PAD,...  3.07 us
  transfers between devices with their start and end apart: 5, of which 2 were waited for; matrix products, arithmetic and copies ran while one was open for 2% of the time, Pallas kernels for 37%

commit v1 on v0

v1 whole, which is shorter than its diff:
```python
import functools

import jax
import jax.numpy as jnp
import numpy as np
from jax import lax
from jax.experimental import pallas as pl
from jax.experimental.pallas import tpu as pltpu
from jax.sharding import PartitionSpec as P


ELEMS = 24
DEGREE = 3
FIELDS = 4
LOCAL = DEGREE + 1
NODES = 4
BASIS = ELEMS + DEGREE
QUAD = ELEMS * NODES
PAD = 32
WIN = LOCAL * PAD
SPAN = NODES * QUAD
GROUPS = ELEMS // 4
WIDE = (GROUPS + 1) * WIN
FLAT = 768
GROUP_ROWS = 4 * PAD

stabilize = 0.25
f32 = jnp.float32
bf16 = jnp.bfloat16
gauss_points_four = [
    -0.8611363115940526,
    -0.3399810435848563,
    0.3399810435848563,
    0.8611363115940526,
]
gauss_weights_four = [
    0.3478548451374538,
    0.6521451548625461,
    0.6521451548625461,
    0.3478548451374538,
]


def spline_tables(knot_list, points, degree):
    current = np.where(
        (knot_list[None, :-1] <= points[:, None]) & (points[:, None] < knot_list[None, 1:]),
        1.0,
        0.0,
    )
    previous = current
    for order_k in range(1, degree + 1):
        previous = current
        amount = len(knot_list) - 1 - order_k
        current = np.zeros((points.shape[0], amount))
        for column in range(amount):
            left_span = knot_list[column + order_k] - knot_list[column]
            right_span = knot_list[column + order_k + 1] - knot_list[column + 1]
            if left_span > 0:
                current[:, column] += (points - knot_list[column]) / left_span * previous[:, column]
            if right_span > 0:
                current[:, column] += (
                    (knot_list[column + order_k + 1] - points)
                    / right_span
                    * previous[:, column + 1]
                )
    slope_part = np.zeros(current.shape)
    for column in range(current.shape[1]):
        left_span = knot_list[column + degree] - knot_list[column]
        right_span = knot_list[column + degree + 1] - knot_list[column + 1]
        if left_span > 0:
            slope_part[:, column] += degree / left_span * previous[:, column]
        if right_span > 0:
            slope_part[:, column] -= degree / right_span * previous[:, column + 1]
    return current, slope_part


def halves(table):
    high = table.astype(np.dtype(bf16)).astype(np.float64)
    return high, table - high


def padded(table, rows, cols):
    out = np.zeros((rows, cols))
    out[: table.shape[0], : table.shape[1]] = table
    return out


@functools.cache
def constants():
    nodes = np.array(gauss_points_four)
    points = (np.arange(ELEMS)[:, None] + (nodes[None, :] + 1.0) / 2.0).reshape(-1)
    weights = np.tile(np.array(gauss_weights_four) / 2.0, ELEMS)
    open_knots = np.concatenate(
        [np.zeros(DEGREE), np.arange(ELEMS + 1.0), np.full(DEGREE, float(ELEMS))]
    )
    even_knots = np.arange(-DEGREE, ELEMS + DEGREE + 1.0)
    value, slope = spline_tables(open_knots, points, DEGREE)
    even_value, even_slope = spline_tables(even_knots, points, DEGREE)
    change = np.round(np.linalg.lstsq(even_value, value, rcond=None)[0] * 4.0) / 4.0
    local_value = even_value[4 * NODES : 5 * NODES, 4 : 4 + LOCAL]
    local_slope = even_slope[4 * NODES : 5 * NODES, 4 : 4 + LOCAL]
    local_w = weights[:NODES, None]

    def kron(local, table):
        wide = padded(table, QUAD, PAD)
        return np.einsum("bj,ck->jkbc", local, wide).reshape(WIN, SPAN)

    ahead = np.concatenate(
        [kron(local_value, value), kron(local_slope, value), kron(local_value, slope)], axis=1
    )
    value_w, slope_w = value * weights[:, None], slope * weights[:, None]
    back = np.concatenate(
        [
            kron(local_value * local_w, value_w).T,
            kron(local_slope * local_w, value_w).T,
            kron(local_value * local_w, slope_w).T,
        ],
        axis=0,
    )
    ahead_high, ahead_low = halves(ahead)
    ahead3 = np.concatenate([ahead_high, ahead_high, ahead_low], axis=0)
    back_high, back_low = halves(back)
    back2 = np.concatenate([back_high, back_low], axis=1)

    def left3(table):
        high, low = halves(padded(table, QUAD, PAD))
        return np.concatenate([high, high, low], axis=1)

    def left4(table):
        high, low = halves(padded(table, QUAD, PAD).T)
        return np.concatenate(
            [np.concatenate([high, high], axis=1), np.concatenate([low, low], axis=1)], axis=0
        )

    spread = np.zeros((BASIS, BASIS, WIDE // PAD, PAD))
    for k in range(BASIS):
        spread[:, k, :BASIS, k] = change.T
    spread = padded(spread.reshape(BASIS * BASIS, WIDE), FLAT, WIDE)
    as16 = lambda a: a.astype(np.dtype(bf16))
    return dict(
        ahead=as16(ahead3),
        back=as16(back2),
        outer=as16(np.stack([left3(slope), left3(value)])),
        inner=as16(np.stack([left4(slope_w), left4(value_w)])),
        spread=as16(spread),
    )


def split(x):
    high = x.astype(bf16)
    return high, (x - high.astype(f32)).astype(bf16)


def dot(a, b):
    return jnp.dot(a, b, preferred_element_type=f32)


def dot_nt(a, b):
    return lax.dot_general(a, b, (((1,), (1,)), ((), ())), preferred_element_type=f32)


def expand(fields, spread):
    parts = []
    for field in fields:
        parts.extend(split(field))
    out = dot(jnp.concatenate(parts, axis=0), spread)
    return halves_sum(out, len(fields))


def halves_sum(out, count):
    return [
        out[2 * n * PAD : (2 * n + 1) * PAD] + out[(2 * n + 1) * PAD : (2 * n + 2) * PAD]
        for n in range(count)
    ]


def shifts(wide):
    rolled = [wide] + [pltpu.roll(wide, WIDE - PAD * r, axis=1) for r in range(1, 4)]
    return [split(x) for x in rolled]


def windows(shifted, m):
    rows = []
    for r in range(4):
        high = shifted[r][0][:, m * WIN : (m + 1) * WIN]
        low = shifted[r][1][:, m * WIN : (m + 1) * WIN]
        rows.append(jnp.concatenate([high, low, high], axis=1))
    return jnp.concatenate(rows, axis=0)


def overlap(rows, groups):
    first, count = groups[0], len(groups)
    total = None
    for r in range(4):
        pieces = []
        if first > 0:
            pieces.append(jnp.zeros((PAD, first * WIN), f32))
        pieces.extend(rows[n][r * PAD : (r + 1) * PAD] for n in range(count))
        rest = WIDE // WIN - first - count
        pieces.append(jnp.zeros((PAD, rest * WIN), f32))
        line = jnp.concatenate(pieces, axis=1)
        if r > 0:
            line = pltpu.roll(line, PAD * r, axis=1)
        total = line if total is None else total + line
    return total


def gather_back(heads_ref, n, back):
    high = heads_ref[n * GROUP_ROWS : (n + 1) * GROUP_ROWS, :]
    low = heads_ref[heads_ref.shape[0] // 2 + n * GROUP_ROWS : heads_ref.shape[0] // 2 + (n + 1) * GROUP_ROWS, :]
    out = dot(jnp.concatenate([high, low], axis=0), back)
    out = out[:GROUP_ROWS] + out[GROUP_ROWS:]
    return out[:, :WIN] + out[:, WIN:]


def load_flat(dst, src):
    dst[...] = jnp.zeros(dst.shape, f32)
    for i in range(BASIS):
        dst[i : i + 1, : BASIS * BASIS] = src[i]


def element_pairs(groups, ahead, outers, inners, planes, back, weight_ref, base, mid_h, mid_l, prod, heads):
    count = len(groups)
    pairs = 2 * count
    half = heads.shape[0] // 2
    done = []

    def forward(p):
        scale = [weight_ref[:, base + (2 * p + q) * SPAN : base + (2 * p + q + 1) * SPAN] for q in range(2)]
        column = 0
        for outer, sources in zip(outers, planes):
            pieces = []
            for q in range(2):
                row = (2 * p + q) * PAD
                for source in sources:
                    stack = []
                    for block in source:
                        cols = slice(block * SPAN, (block + 1) * SPAN)
                        stack += [mid_h[row : row + PAD, cols], mid_l[row : row + PAD, cols], mid_h[row : row + PAD, cols]]
                    pieces.append(jnp.concatenate(stack, axis=0))
            out = dot(outer, jnp.concatenate(pieces, axis=1))
            wide = jnp.concatenate([scale[q] for q in range(2) for _ in sources], axis=1)
            high, low = split(out * wide)
            width = 2 * len(sources) * SPAN
            prod[p % 2, :QUAD, column : column + width] = high
            prod[p % 2, QUAD:, column : column + width] = low
            column += width

    def backward(p):
        column = 0
        place = 0
        for inner, sources in zip(inners, planes):
            width = 2 * len(sources) * SPAN
            out = dot(inner, prod[p % 2, :, column : column + width])
            high, low = split(out[:PAD] + out[PAD:])
            for q in range(2):
                row = (2 * p + q) * PAD
                take = slice(q * len(sources) * SPAN, (q + 1) * len(sources) * SPAN)
                put = slice(place, place + len(sources) * SPAN)
                heads[row : row + PAD, put] = high[:, take]
                heads[half + row : half + row + PAD, put] = low[:, take]
            column += width
            place += len(sources) * SPAN

    ahead(0)
    for p in range(pairs + 1):
        if p < pairs:
            forward(p)
            if p % 2 == 0 and p // 2 + 1 < count:
                ahead(p // 2 + 1)
        if p > 0:
            backward(p - 1)
        if p >= 3 and p % 2 == 1:
            done.append(gather_back(heads, len(done), back))
    while len(done) < count:
        done.append(gather_back(heads, len(done), back))
    return overlap(done, groups)


def start_all(pairs, sems):
    copies = [pltpu.make_async_copy(src, dst, sems.at[n]) for n, (src, dst) in enumerate(pairs)]
    for copy in copies:
        copy.start()
    return copies


def stiff_kernel(groups, fetch_lanes, wide_ref, ahead_ref, outer_ref, inner_ref, back_ref, weight_ref, next_hbm, out_ref, next_ref, mid_h, mid_l, prod, heads, sems):
    copies = start_all([(next_hbm.at[0, :, fetch_lanes], next_ref)], sems)
    shifted = shifts(wide_ref[...])

    def ahead(n):
        high, low = split(dot(windows(shifted, groups[n]), ahead_ref[...]))
        mid_h[n * GROUP_ROWS : (n + 1) * GROUP_ROWS, :] = high
        mid_l[n * GROUP_ROWS : (n + 1) * GROUP_ROWS, :] = low

    out_ref[...] = element_pairs(
        groups,
        ahead,
        (outer_ref[0], outer_ref[1]),
        (inner_ref[0], inner_ref[1]),
        (((0,),), ((1,), (2,))),
        back_ref[...],
        weight_ref,
        0,
        mid_h,
        mid_l,
        prod,
        heads,
    )
    for copy in copies:
        copy.wait()


def volume_kernel(near_ref, far_ref, spread_ref, ahead_ref, outer_ref, inner_ref, back_ref, weight_ref, stiff_a, stiff_b, out_ref, flat, mid_h, mid_l, prod, heads):
    groups = list(range(GROUPS))
    sub = lax.axis_index("sub")
    is_pressure = sub == FIELDS - 1
    load_flat(flat.at[0], near_ref)
    load_flat(flat.at[1], far_ref.at[0])
    load_flat(flat.at[2], far_ref.at[1])
    chosen = jnp.where(is_pressure, 2, 2 - sub)
    zero = jnp.zeros((PAD, FLAT), f32)
    fields = [
        flat[chosen],
        jnp.where(is_pressure, flat[1], zero),
        jnp.where(is_pressure, flat[0], zero),
    ]
    shifted = [shifts(wide) for wide in expand(fields, spread_ref[...])]

    def ahead(n):
        at = slice(n * GROUP_ROWS, (n + 1) * GROUP_ROWS)
        mid = dot(windows(shifted[0], groups[n]), ahead_ref[:, :SPAN])
        high, low = split(mid)
        mid_h[at, :SPAN] = high
        mid_l[at, :SPAN] = low
        mid = dot(windows(shifted[1], groups[n]), ahead_ref[:, SPAN : 2 * SPAN]) + dot(
            windows(shifted[2], groups[n]), ahead_ref[:, 2 * SPAN :]
        )
        high, low = split(mid)
        mid_h[at, SPAN:] = high
        mid_l[at, SPAN:] = low

    along = jnp.where(is_pressure, 0, 1)
    outer = jnp.concatenate([outer_ref[along], outer_ref[1]], axis=1)
    inner = inner_ref[jnp.where(sub == 0, 0, 1)]
    kind = jnp.where(is_pressure, 0, sub)
    back = back_ref[pl.ds(pl.multiple_of(kind * SPAN, SPAN), SPAN), :]
    volume = element_pairs(
        groups, ahead, (outer,), (inner,), (((0, 1),),), back, weight_ref, 0, mid_h, mid_l, prod, heads
    )
    factor = jnp.where(is_pressure, -stabilize, 1.0).astype(f32)
    total = factor * (stiff_a[...] + stiff_b[...]) - volume
    out = dot_nt(jnp.concatenate(split(total), axis=0), spread_ref[...])
    out_ref[...] = out[:PAD] + out[PAD:]


def masked(matrix, limit):
    rows = lax.broadcasted_iota(jnp.int32, matrix.shape, 0)
    return jnp.where(rows < limit, matrix, 0.0)


def layers():
    lanes = lax.broadcasted_iota(jnp.int32, (PAD, FLAT), 1)
    group = jnp.floor((lanes.astype(f32) + 0.5) * (1.0 / BASIS)).astype(jnp.int32)
    rows = lax.broadcasted_iota(jnp.int32, (PAD, FLAT), 0)
    inside = lanes - BASIS * group == rows
    return group, rows, jnp.where(inside, 1.0, 0.0).astype(bf16)


def dot_split(a, b, dims):
    a_high, a_low = split(a)
    b_high, b_low = split(b)
    dims = (dims, ((), ()))
    general = functools.partial(lax.dot_general, dimension_numbers=dims, preferred_element_type=f32)
    return general(a_high, b_high) + (general(a_high, b_low) + general(a_low, b_high))


def prep_kernel(links_hbm, field_hbm, lag_hbm, mortar_hbm, spread_hbm, ahead_hbm, outer_hbm, inner_hbm, back_hbm, weight_hbm, own_ref, wide_ref, spread_ref, ahead_ref, outer_ref, inner_ref, back_ref, weight_ref, links, field, lag, mortar, flat, line, sems):
    copies = start_all(
        [
            (field_hbm, field),
            (lag_hbm, lag),
            (links_hbm, links),
            (mortar_hbm, mortar),
            (spread_hbm, spread_ref),
            (ahead_hbm, ahead_ref),
            (outer_hbm, outer_ref),
            (inner_hbm, inner_ref),
            (back_hbm, back_ref),
            (weight_hbm.at[0, :, pl.ds(0, weight_ref.shape[1])], weight_ref),
        ],
        sems,
    )
    slots = lag.shape[0]
    own_ref[...] = jnp.zeros(own_ref.shape, f32)
    line[...] = jnp.zeros(line.shape, f32)
    group, rows, fold = layers()
    same = rows == group
    for copy in copies[:4]:
        copy.wait()
    load_flat(flat, field)
    for s in range(slots):
        line[s : s + 1, : BASIS * BASIS] = lag[s, 0]
    spreads = [jnp.where(same, line[s : s + 1, :], 0.0) for s in range(slots)]
    spreads += [
        jnp.where(same, flat[0:1, :], 0.0),
        jnp.where(same, flat[BASIS - 1 : BASIS, :], 0.0),
        jnp.where(group == 0, flat[...], 0.0),
        jnp.where(group == BASIS - 1, flat[...], 0.0),
    ]
    parts = []
    for x in spreads:
        parts.extend(split(x))
    squares = halves_sum(dot_nt(jnp.concatenate(parts, axis=0), fold), 4 + slots)
    base = lax.axis_index("patch") * slots
    halfway = []
    for s in range(slots):
        for side in range(2):
            left = masked(mortar[s, side, :, 0, :], links[4, base + s])
            halfway.append(dot_split(left, squares[s][:BASIS, :BASIS], ((0,), (0,))))
    for s in range(slots):
        for side in range(2):
            right = masked(mortar[s, side, :, 1, :], links[5, base + s])
            both = dot_split(halfway[2 * s + side], right, ((1,), (0,)))
            item = 2 * s + side
            at = (item % 4) * PAD
            own_ref[1 + item // 4, :BASIS, at : at + BASIS] = both if side == 0 else -both
    for f in range(4):
        own_ref[0, :, f * PAD : (f + 1) * PAD] = squares[slots + f]
    copies[4].wait()
    (wide,) = expand([flat[...]], spread_ref[...])
    wide_ref[...] = wide
    for copy in copies[5:]:
        copy.wait()


def position(mine, other, masks):
    differ = jnp.bitwise_xor(mine, other)
    total = jnp.int32(0)
    for n, mask in enumerate(masks):
        total = total + jnp.where(jnp.bitwise_and(differ, mask) != 0, jnp.int32(1 << n), jnp.int32(0))
    return total


def final_kernel(masks, links_hbm, mortar_hbm, *refs):
    rounds = len(masks)
    part_refs = refs[: rounds + 1]
    inner_ref, out_ref, jump_ref, buf, links, mortar, found, sems = refs[rounds + 1 :]
    copies = start_all([(links_hbm, links), (mortar_hbm, mortar)], sems)
    slots = mortar.shape[0]
    mine = lax.axis_index("patch")
    table = links.shape[1]
    buf[0] = part_refs[0][...]
    for n in range(rounds):
        buf[(1 << n) : (2 << n)] = part_refs[n + 1][...].reshape((1 << n,) + buf.shape[1:])
    group, rows, fold = layers()
    same = rows == group
    for f in range(5):
        found[f] = 0
    for copy in copies:
        copy.wait()

    def look(t, carry):
        for side in range(2):
            hit = jnp.logical_and(links[side, t] == mine, links[4, t] > 0)
            found[jnp.where(hit, links[2 + side, t], 4)] = 2 * t + side
        return carry

    def pick(owner, plane, lane):
        block = buf[position(mine, owner, masks), plane]
        return pltpu.roll(block, lax.rem(WIN - lane * PAD, WIN), axis=1)[:, :PAD]

    base = mine * slots
    halfway = []
    for s in range(slots):
        for side in range(2):
            trace = pick(links[side, base + s], 0, links[2 + side, base + s])
            left = masked(mortar[s, side, :, 0, :], links[4, base + s])
            halfway.append(dot_split(left, trace[:BASIS, :BASIS], ((1,), (0,))))
    jumps = []
    for s in range(slots):
        total = None
        for side in range(2):
            right = masked(mortar[s, side, :, 1, :], links[5, base + s])
            both = dot_split(halfway[2 * s + side], right, ((1,), (1,)))
            total = both if total is None else total - both
        jumps.append(jnp.pad(total, ((0, PAD - BASIS), (0, PAD - BASIS))))
    if table <= 64:
        for t in range(table):
            look(t, 0)
    else:
        lax.fori_loop(0, table, look, 0, unroll=8)
    squares = []
    for f in range(4):
        item = found[f]
        owner = lax.div(item, 2 * slots)
        item = lax.rem(item, 2 * slots)
        squares.append(pick(owner, 1 + lax.div(item, 4), lax.rem(item, 4)))
    parts = []
    for x in squares + jumps:
        parts.extend(split(x))
    lines = halves_sum(dot(jnp.concatenate(parts, axis=0), fold), 4 + slots)
    out = inner_ref[...]
    low_row = jnp.sum(jnp.where(same, lines[0], 0.0), axis=0, keepdims=True)
    high_row = jnp.sum(jnp.where(same, lines[1], 0.0), axis=0, keepdims=True)
    out = out + jnp.where(rows == 0, low_row, 0.0) + jnp.where(rows == BASIS - 1, high_row, 0.0)
    out = out + jnp.where(group == 0, lines[2], 0.0) + jnp.where(group == BASIS - 1, lines[3], 0.0)
    for i in range(BASIS):
        out_ref[i] = out[i : i + 1, : BASIS * BASIS]
    for s in range(slots):
        row = jnp.sum(jnp.where(same, lines[4 + s], 0.0), axis=0, keepdims=True)
        jump_ref[s, 0] = row[:, : BASIS * BASIS]


def vmem():
    return pl.BlockSpec(memory_space=pltpu.VMEM)


def anywhere():
    return pl.BlockSpec(memory_space=pltpu.HBM)


def in_hbm(*arrays):
    return [pltpu.with_memory_space_constraint(x, pltpu.HBM) for x in arrays]


params = pltpu.CompilerParams(vmem_limit_bytes=24 << 20)
halfspan = (GROUPS // 2) * 4 * SPAN


def stiff_call(groups, fetch, wide, tables, weight, following):
    count = 4 * len(groups)
    lanes = pl.ds(fetch[0], fetch[1])
    return pl.pallas_call(
        functools.partial(stiff_kernel, groups, lanes),
        out_shape=(
            jax.ShapeDtypeStruct((PAD, WIDE), f32),
            jax.ShapeDtypeStruct((QUAD, fetch[1]), f32),
        ),
        in_specs=[vmem()] * 6 + [anywhere()],
        out_specs=(vmem(), vmem()),
        scratch_shapes=[
            pltpu.VMEM((count * PAD, 3 * SPAN), bf16),
            pltpu.VMEM((count * PAD, 3 * SPAN), bf16),
            pltpu.VMEM((2, 2 * QUAD, 6 * SPAN), bf16),
            pltpu.VMEM((2 * count * PAD, 3 * SPAN), bf16),
            pltpu.SemaphoreType.DMA((1,)),
        ],
        compiler_params=params,
    )(wide, *tables[1:], weight, *in_hbm(following))


def volume_call(near, far, tables, weight, stiff_a, stiff_b):
    return pl.pallas_call(
        volume_kernel,
        out_shape=jax.ShapeDtypeStruct((PAD, FLAT), f32),
        in_specs=[vmem()] * 10,
        out_specs=vmem(),
        scratch_shapes=[
            pltpu.VMEM((3, PAD, FLAT), f32),
            pltpu.VMEM((ELEMS * PAD, 2 * SPAN), bf16),
            pltpu.VMEM((ELEMS * PAD, 2 * SPAN), bf16),
            pltpu.VMEM((2, 2 * QUAD, 2 * SPAN), bf16),
            pltpu.VMEM((2 * ELEMS * PAD, SPAN), bf16),
        ],
        compiler_params=params,
    )(near, far, *tables, weight, stiff_a, stiff_b)


def prep_call(links, field, lagrange, mortar, tables, stiff_weight, planes):
    return pl.pallas_call(
        prep_kernel,
        out_shape=(
            jax.ShapeDtypeStruct((planes, PAD, WIN), f32),
            jax.ShapeDtypeStruct((PAD, WIDE), f32),
            *(jax.ShapeDtypeStruct(t.shape, bf16) for t in tables),
            jax.ShapeDtypeStruct((QUAD, halfspan), f32),
        ),
        in_specs=[anywhere()] * 10,
        out_specs=(vmem(),) * 8,
        scratch_shapes=[
            pltpu.SMEM(links.shape, jnp.int32),
            pltpu.VMEM(field.shape, f32),
            pltpu.VMEM(lagrange.shape, f32),
            pltpu.VMEM(mortar.shape, f32),
            pltpu.VMEM((PAD, FLAT), f32),
            pltpu.VMEM((8, FLAT), f32),
            pltpu.SemaphoreType.DMA((10,)),
        ],
        compiler_params=params,
    )(*in_hbm(links, field, lagrange, mortar, *tables, stiff_weight))


def swap(array, axis, mask):
    size = lax.axis_size(axis)
    return lax.ppermute(array, axis, [(n, n ^ mask) for n in range(size)])


def after(array, *others):
    return lax.optimization_barrier((array,) + others)[0]


def per_device(state, stiff_weight, volume_weight, lagrange, mortar, links):
    tables = [jnp.asarray(constants()[name]) for name in ("spread", "ahead", "outer", "inner", "back")]
    patches = lax.axis_size("patch")
    slots = mortar.shape[0]
    planes = 1 + (2 * slots + 3) // 4
    masks = [1 << n for n in reversed(range(patches.bit_length() - 1))]
    field = jnp.transpose(state, (0, 1, 3, 2, 4))[0, 0]
    mortar = jnp.transpose(mortar, (0, 1, 3, 2, 4))
    links = links.T

    near = swap(field, "sub", 1)
    own, wide, *tables, weight_a = prep_call(links, field, lagrange, mortar, tables, stiff_weight, planes)
    far = swap(jnp.stack([field, near]), "sub", 2)
    first = GROUPS // 2
    stiff_a, weight_b = stiff_call(
        list(range(first)), (halfspan, ELEMS * SPAN - halfspan), wide, tables, weight_a, stiff_weight
    )
    stiff_b, weight_c = stiff_call(
        list(range(first, GROUPS)), (0, ELEMS * SPAN), wide, tables, weight_b, volume_weight
    )
    inner = volume_call(near, far, tables, weight_c, stiff_a, stiff_b)
    gates = [None, stiff_a, stiff_b]
    parts = [own]
    held = own
    for n, mask in enumerate(masks):
        late = len(masks) - n
        gate = gates[max(0, 3 - late)] if n > 0 else None
        other = swap(held if gate is None else after(held, gate), "patch", mask)
        parts.append(other)
        held = jnp.concatenate([held, other], axis=0)
    residual, constraint = pl.pallas_call(
        functools.partial(final_kernel, masks),
        out_shape=(
            jax.ShapeDtypeStruct(field.shape, f32),
            jax.ShapeDtypeStruct((slots, 1, 1, BASIS * BASIS), f32),
        ),
        in_specs=[anywhere(), anywhere()] + [vmem()] * (len(parts) + 1),
        out_specs=(vmem(), vmem()),
        scratch_shapes=[
            pltpu.VMEM((patches, planes, PAD, WIN), f32),
            pltpu.SMEM(links.shape, jnp.int32),
            pltpu.VMEM(mortar.shape, f32),
            pltpu.SMEM((8,), jnp.int32),
            pltpu.SemaphoreType.DMA((2,)),
        ],
        compiler_params=params,
    )(*in_hbm(links, mortar), *parts, inner)
    return jnp.transpose(residual[None, None], (0, 1, 3, 2, 4)), constraint


def solution(mesh):
    return jax.shard_map(
        per_device,
        mesh=mesh,
        in_specs=(
            P("patch", "sub", None, None, None),
            P("patch", None, None),
            P("patch", None, None),
            P("patch", "sub", None, None),
            P("patch", None, None, None, None),
            P(),
        ),
        out_specs=(P("patch", "sub", None, None, None), P("patch", "sub", None, None)),
        check_vma=False,
    )
```

time: 53 us -> 30 us (0.57)
  local copies, waits for them, and re-layouts: 11.9 us -> 0.01 us
  Pallas kernels: 25.8 us -> 15.1 us
    unnamed x27 -> x2, local copies, waits for them, and re-layouts: 10.2 us -> 0.01 us
    pallas_call x4, Pallas kernels: 22.7 us -> 12.7 us  [the longest x2 6.03 us: stiff_call(): pl.pallas_call(functools.partial(stiff_kernel, groups, lanes), out_shape=...]
    squeeze x1 -> x0, local copies, waits for them, and re-layouts: 0.97 us -> none  [per_device(): far = swap(jnp.concatenate([state[0, 0], near[0, 0]], axis=0), 'sub', 2)]
    pallas_call x1, Pallas kernels: 3.15 us -> 2.36 us  [per_device(): pl.pallas_call(functools.partial(final_kernel, masks), out_shape=(jax.Sha...]
    pallas_call x1 -> x0, local copies, waits for them, and re-layouts: 0.72 us -> none  [per_device(): pl.pallas_call(functools.partial(final_kernel, masks), out_shape=(jax.Sha...]
  transfers between devices with their start and end apart: 5 -> 5, of which waited for: 2 -> 1; matrix products, arithmetic and copies ran while one was open for 2% -> 1% of each run, Pallas kernels for 37% -> 34%
where the time goes in v1:
time: 30 us; the launch traced here: 29.8 us
  Pallas kernels  15.1 us (50%)
  starting transfers between devices  8.92 us (30%)
  waiting for transfers between devices  4.91 us (16%)
  between operations  0.68 us (2%)
    ppermute x5, starting transfers between devices, swap(): return lax.ppermute(array, axis, [(n, n ^ mask) for n in range(size)])  8.92 us
    pallas_call x2, Pallas kernels, stiff_call(): pl.pallas_call(functools.partial(stiff_kernel, groups, lanes), out_shape=...  6.03 us
    ppermute x5, waiting for transfers between devices, swap(): return lax.ppermute(array, axis, [(n, n ^ mask) for n in range(size)])  4.91 us
    pallas_call x1, Pallas kernels, volume_call(): pl.pallas_call(volume_kernel, out_shape=jax.ShapeDtypeStruct((PAD, FLAT),...  4.04 us
    pallas_call x1, Pallas kernels, prep_call(): pl.pallas_call(prep_kernel, out_shape=(jax.ShapeDtypeStruct((planes, PAD,...  2.66 us
    pallas_call x1, Pallas kernels, per_device(): pl.pallas_call(functools.partial(final_kernel, masks), out_shape=(jax.Sha...  2.36 us
  transfers between devices with their start and end apart: 5, of which 1 were waited for; matrix products, arithmetic and copies ran while one was open for 1% of the time, Pallas kernels for 34%

profile of v1, /device:TPU:0, one launch (start us, length us, event | category | flops | bytes accessed | tf_op | source)
XLA Modules:
  0.0 29.8 jit_solution(17933668414444188412)
XLA Ops:
  0.6 2.7 %shard_map.122 = (f32[3,32,128]{2,1,0:T(8,128)S(1)}, f32[32,896]{1,0:T(8,128)S(1)}, bf16[768,896]{1,0:T(8,128)(2,1)S(1)}, bf16[384,1152]{1,0:T(8,128)(2,1)S(1)},...) custom-call(s32[6,32]{1,0:T(8,128)} %bitcast.14, ...), custom_call_target="tpu_custom_call" | custom-call | tf_op jit(solution)/shard_map/pallas_call | solution.py:571
  3.3 4.1 %collective-permute-start = (f32[3,32,128]{2,1,0:T(8,128)S(1)}, f32[3,32,128]{2,1,0:T(8,128)S(1)}, u32[]{:S(2)}, u32[]{:S(2)}) collective-permute-start(f32[3,32,128]{2,1,0:T(8,128)S(1)} %get-tuple-element.18.refs_0_), channel_id=1, source_target_pairs={{0,16},{4,20},{8,24},{12,28},{16,0},{20,4},{24,8},{28,12},{1,17},{... | collective-permute-start | bytes 147464 | tf_op jit(solution)/shard_map/ppermute | solution.py:596
  7.4 0.0 copy-start
  7.4 3.0 %shard_map.123 = (f32[32,896]{1,0:T(8,128)S(1)}, f32[96,4608]{1,0:T(8,128)S(1)}) custom-call(f32[32,896]{1,0:T(8,128)S(1)} %get-tuple-element.19.wide_ref, bf16[384,1152]{1,0:T(8,128)(2,1)S(1)} %get-tuple-element.20.ahead_ref, bf16[2,96,96]{2,1,0:T(8,128)(2,1)S(1)} %get-tuple-element.21.outer_ref, bf16[2,64,192]{2,1,0:T(8,128)(2,1)S(1)} %get-tuple-element.22.inner_ref, ...), custom_call_target="tpu_custom_call" | custom-call | tf_op jit(solution)/shard_map/pallas_call | solution.py:534
  10.5 0.0 collective-permute-done.refs_1_
  10.5 1.6 %collective-permute-start.1 = (f32[6,32,128]{2,1,0:T(8,128)S(1)}, f32[6,32,128]{2,1,0:T(8,128)S(1)}, u32[]{:S(2)}, u32[]{:S(2)}) collective-permute-start(f32[6,32,128]{2,1,0:T(8,128)S(1)} %pad_maximum_fusion.2), channel_id=1, source_target_pairs={{0,8},{4,12},{8,0},{12,4},{16,24},{20,28},{24,16},{28,20},{1,9},{5... | collective-permute-start | bytes 294920 | tf_op jit(solution)/shard_map/ppermute | solution.py:596
  12.1 0.0 copy-done
  12.1 0.0 collective-permute-start.3
  12.1 3.0 %shard_map.124 = (f32[32,896]{1,0:T(8,128)S(1)}, f32[96,9216]{1,0:T(8,128)S(1)}) custom-call(f32[32,896]{1,0:T(8,128)S(1)} %get-tuple-element.19.wide_ref, bf16[384,1152]{1,0:T(8,128)(2,1)S(1)} %get-tuple-element.20.ahead_ref, bf16[2,96,96]{2,1,0:T(8,128)(2,1)S(1)} %get-tuple-element.21.outer_ref, bf16[2,64,192]{2,1,0:T(8,128)(2,1)S(1)} %get-tuple-element.22.inner_ref, ...), custom_call_target="tpu_custom_call" | custom-call | tf_op jit(solution)/shard_map/pallas_call | solution.py:534
  15.1 0.0 collective-permute-done.1.refs_2_
  15.2 1.6 %collective-permute-start.2 = (f32[12,32,128]{2,1,0:T(8,128)S(1)}, f32[12,32,128]{2,1,0:T(8,128)S(1)}, u32[]{:S(2)}, u32[]{:S(2)}) collective-permute-start(f32[12,32,128]{2,1,0:T(8,128)S(1)} %pad_maximum_fusion), channel_id=1, source_target_pairs={{0,4},{4,0},{8,12},{12,8},{16,20},{20,16},{24,28},{28,24},{1,5},{5... | collective-permute-start | bytes 589832 | tf_op jit(solution)/shard_map/ppermute | solution.py:596
  16.8 0.0 collective-permute-done.3.near_ref
  16.8 0.1 pad_maximum_fusion.1
  16.9 1.6 %collective-permute-start.4 = (f32[2,27,1,729]{3,2,1,0:T(1,128)S(1)}, f32[2,27,1,729]{3,2,1,0:T(1,128)S(1)}, u32[]{:S(2)}, u32[]{:S(2)}) collective-permute-start(f32[2,27,1,729]{3,2,1,0:T(1,128)S(1)} %pad_maximum_fusion.1), channel_id=1, source_target_pairs={{0,2},{1,3},{2,0},{3,1},{4,6},{5,7},{6,4},{7,5},{8,10},{9,11},{10,... | collective-permute-start | bytes 472400 | tf_op jit(solution)/shard_map/ppermute | solution.py:596
  18.5 4.9 %collective-permute-done.4.far_ref = f32[2,27,1,729]{3,2,1,0:T(1,128)S(1)} collective-permute-done((f32[2,27,1,729]{3,2,1,0:T(1,128)S(1)}, f32[2,27,1,729]{3,2,1,0:T(1,128)S(1)}, u32[]{:S(2)}, u32[]{:S(2)}) %collective-permute-start.4) | collective-permute-done | bytes 157496 | tf_op jit(solution)/shard_map/ppermute | solution.py:596
  23.4 4.0 %shard_map.125.refs_4_ = f32[32,768]{1,0:T(8,128)S(1)} custom-call(f32[27,1,729]{2,1,0:T(1,128)S(1)} %collective-permute-done.3.near_ref, f32[2,27,1,729]{3,2,1,0:T(1,128)S(1)} %collective-permute-done.4.far_ref, bf16[768,896]{1,0:T(8,128)(2,1)S(1)} %get-tuple-element.30.spread_ref, bf16[384,1152]{1,0:T(8,128)(2,1)S(1)} %get-tuple-element.20.ahead_ref, ...), custom_call_target="tpu_custom_call" | custom-call | tf_op jit(solution)/shard_map/pallas_call | solution.py:554
  27.4 0.0 collective-permute-done.2.refs_3_
  27.4 2.4 %shard_map.126 = (f32[27,1,729]{2,1,0:T(1,128)}, f32[4,1,1,729]{3,2,1,0:T(1,128)}) custom-call(s32[6,32]{1,0:T(8,128)} %bitcast.15, f32[4,2,27,2,27]{4,3,2,1,0:T(2,128)} %bitcast.10, f32[3,32,128]{2,1,0:T(8,128)S(1)} %get-tuple-element.18.refs_0_, f32[3,32,128]{2,1,0:T(8,128)S(1)} %collective-permute-done.refs_1_, ...), custom_call_target="tpu_custom_call" | custom-call | tf_op jit(solution)/shard_map/pallas_call | solution.py:633
  (2 shorter events, 0.0 us)
Async XLA Ops:
  3.3 7.2 %collective-permute-start = (f32[3,32,128]{2,1,0:T(8,128)S(1)}, f32[3,32,128]{2,1,0:T(8,128)S(1)}, u32[]{:S(2)}, u32[]{:S(2)}) collective-permute-start(f32[3,32,128]{2,1,0:T(8,128)S(1)} %get-tuple-element.18.refs_0_), channel_id=1, source_target_pairs={{0,16},{4,20},{8,24},{12,28},{16,0},{20,4},{24,8},{28,12},{1,17},{... | collective-permute-start | bytes 147464 | tf_op jit(solution)/shard_map/ppermute | solution.py:596
  7.4 4.7 %copy-start = (f32[1,1,1,27,729]{4,2,3,1,0:T(1,128)S(1)}, f32[1,1,1,27,729]{4,2,3,1,0:T(1,128)}, u32[]{:S(2)}) copy-start(f32[1,1,1,27,729]{4,2,3,1,0:T(1,128)} %param.11) | copy-start | bytes 236200
  10.5 4.7 %collective-permute-start.1 = (f32[6,32,128]{2,1,0:T(8,128)S(1)}, f32[6,32,128]{2,1,0:T(8,128)S(1)}, u32[]{:S(2)}, u32[]{:S(2)}) collective-permute-start(f32[6,32,128]{2,1,0:T(8,128)S(1)} %pad_maximum_fusion.2), channel_id=1, source_target_pairs={{0,8},{4,12},{8,0},{12,4},{16,24},{20,28},{24,16},{28,20},{1,9},{5... | collective-permute-start | bytes 294920 | tf_op jit(solution)/shard_map/ppermute | solution.py:596
  12.1 4.7 %collective-permute-start.3 = (f32[27,1,729]{2,1,0:T(1,128)S(1)}, f32[27,1,729]{2,1,0:T(1,128)S(1)}, u32[]{:S(2)}, u32[]{:S(2)}) collective-permute-start(f32[27,1,729]{2,1,0:T(1,128)S(1)} %bitcast.12), channel_id=1, source_target_pairs={{0,1},{1,0},{2,3},{3,2},{4,5},{5,4},{6,7},{7,6},{8,9},{9,8},{10,11... | collective-permute-start | bytes 236204 | tf_op jit(solution)/shard_map/ppermute | solution.py:596
  15.2 12.2 %collective-permute-start.2 = (f32[12,32,128]{2,1,0:T(8,128)S(1)}, f32[12,32,128]{2,1,0:T(8,128)S(1)}, u32[]{:S(2)}, u32[]{:S(2)}) collective-permute-start(f32[12,32,128]{2,1,0:T(8,128)S(1)} %pad_maximum_fusion), channel_id=1, source_target_pairs={{0,4},{4,0},{8,12},{12,8},{16,20},{20,16},{24,28},{28,24},{1,5},{5... | collective-permute-start | bytes 589832 | tf_op jit(solution)/shard_map/ppermute | solution.py:596
  16.9 6.4 %collective-permute-start.4 = (f32[2,27,1,729]{3,2,1,0:T(1,128)S(1)}, f32[2,27,1,729]{3,2,1,0:T(1,128)S(1)}, u32[]{:S(2)}, u32[]{:S(2)}) collective-permute-start(f32[2,27,1,729]{3,2,1,0:T(1,128)S(1)} %pad_maximum_fusion.1), channel_id=1, source_target_pairs={{0,2},{1,3},{2,0},{3,1},{4,6},{5,7},{6,4},{7,5},{8,10},{9,11},{10,... | collective-permute-start | bytes 472400 | tf_op jit(solution)/shard_map/ppermute | solution.py:596

commit v2 on v1

--- a/solution.py
+++ b/solution.py
@@ -20,6 +20,7 @@
 WIN = LOCAL * PAD
 SPAN = NODES * QUAD
 GROUPS = ELEMS // 4
+EARLY = GROUPS - 2
 WIDE = (GROUPS + 1) * WIN
 FLAT = 768
 GROUP_ROWS = 4 * PAD
@@ -219,7 +220,7 @@
         dst[i : i + 1, : BASIS * BASIS] = src[i]
 
 
-def element_pairs(groups, ahead, outers, inners, planes, back, weight_ref, base, mid_h, mid_l, prod, heads):
+def element_pairs(groups, ahead, outers, inners, planes, back, weight_ref, base, mid_h, mid_l, prod, heads, hooks=None):
     count = len(groups)
     pairs = 2 * count
     half = heads.shape[0] // 2
@@ -268,6 +269,8 @@
             forward(p)
             if p % 2 == 0 and p // 2 + 1 < count:
                 ahead(p // 2 + 1)
+        if hooks and p in hooks:
+            hooks[p]()
         if p > 0:
             backward(p - 1)
         if p >= 3 and p % 2 == 1:
@@ -311,8 +314,38 @@
         copy.wait()
 
 
-def volume_kernel(near_ref, far_ref, spread_ref, ahead_ref, outer_ref, inner_ref, back_ref, weight_ref, stiff_a, stiff_b, out_ref, flat, mid_h, mid_l, prod, heads):
-    groups = list(range(GROUPS))
+def volume_tables(outer_ref, inner_ref, back_ref):
+    sub = lax.axis_index("sub")
+    is_pressure = sub == FIELDS - 1
+    outer = jnp.concatenate([outer_ref[jnp.where(is_pressure, 0, 1)], outer_ref[1]], axis=1)
+    inner = inner_ref[jnp.where(sub == 0, 0, 1)]
+    kind = jnp.where(is_pressure, 0, sub)
+    back = back_ref[pl.ds(pl.multiple_of(kind * SPAN, SPAN), SPAN), :]
+    return outer, inner, back
+
+
+def volume_groups(groups, wides, ahead_ref, tables, weight_ref, mid_h, mid_l, prod, heads, hooks=None):
+    shifted = [shifts(wide) for wide in wides]
+    outer, inner, back = tables
+
+    def ahead(n):
+        at = slice(n * GROUP_ROWS, (n + 1) * GROUP_ROWS)
+        m = groups[n]
+        high, low = split(dot(windows(shifted[0], m), ahead_ref[:, :SPAN]))
+        mid_h[at, :SPAN] = high
+        mid_l[at, :SPAN] = low
+        both = jnp.concatenate([windows(shifted[1], m), windows(shifted[2], m)], axis=1)
+        high, low = split(dot(both, jnp.concatenate([ahead_ref[:, SPAN : 2 * SPAN], ahead_ref[:, 2 * SPAN :]], axis=0)))
+        mid_h[at, SPAN:] = high
+        mid_l[at, SPAN:] = low
+
+    base = groups[0] * 4 * SPAN
+    return element_pairs(
+        groups, ahead, (outer,), (inner,), (((0, 1),),), back, weight_ref, base, mid_h, mid_l, prod, heads, hooks
+    )
+
+
+def volume_kernel(groups, near_ref, far_ref, spread_ref, ahead_ref, outer_ref, inner_ref, back_ref, weight_ref, out_ref, wides_ref, flat, mid_h, mid_l, prod, heads):
     sub = lax.axis_index("sub")
     is_pressure = sub == FIELDS - 1
     load_flat(flat.at[0], near_ref)
@@ -325,33 +358,11 @@
         jnp.where(is_pressure, flat[1], zero),
         jnp.where(is_pressure, flat[0], zero),
     ]
-    shifted = [shifts(wide) for wide in expand(fields, spread_ref[...])]
-
-    def ahead(n):
-        at = slice(n * GROUP_ROWS, (n + 1) * GROUP_ROWS)
-        mid = dot(windows(shifted[0], groups[n]), ahead_ref[:, :SPAN])
-        high, low = split(mid)
-        mid_h[at, :SPAN] = high
-        mid_l[at, :SPAN] = low
-        mid = dot(windows(shifted[1], groups[n]), ahead_ref[:, SPAN : 2 * SPAN]) + dot(
-            windows(shifted[2], groups[n]), ahead_ref[:, 2 * SPAN :]
-        )
-        high, low = split(mid)
-        mid_h[at, SPAN:] = high
-        mid_l[at, SPAN:] = low
-
-    along = jnp.where(is_pressure, 0, 1)
-    outer = jnp.concatenate([outer_ref[along], outer_ref[1]], axis=1)
-    inner = inner_ref[jnp.where(sub == 0, 0, 1)]
-    kind = jnp.where(is_pressure, 0, sub)
-    back = back_ref[pl.ds(pl.multiple_of(kind * SPAN, SPAN), SPAN), :]
-    volume = element_pairs(
-        groups, ahead, (outer,), (inner,), (((0, 1),),), back, weight_ref, 0, mid_h, mid_l, prod, heads
-    )
-    factor = jnp.where(is_pressure, -stabilize, 1.0).astype(f32)
-    total = factor * (stiff_a[...] + stiff_b[...]) - volume
-    out = dot_nt(jnp.concatenate(split(total), axis=0), spread_ref[...])
-    out_ref[...] = out[:PAD] + out[PAD:]
+    wides = expand(fields, spread_ref[...])
+    for n in range(3):
+        wides_ref[n] = wides[n]
+    tables = volume_tables(outer_ref, inner_ref, back_ref)
+    out_ref[...] = volume_groups(groups, wides, ahead_ref, tables, weight_ref, mid_h, mid_l, prod, heads)
 
 
 def masked(matrix, limit):
@@ -375,12 +386,57 @@
     return general(a_high, b_high) + (general(a_high, b_low) + general(a_low, b_high))
 
 
-def prep_kernel(links_hbm, field_hbm, lag_hbm, mortar_hbm, spread_hbm, ahead_hbm, outer_hbm, inner_hbm, back_hbm, weight_hbm, own_ref, wide_ref, spread_ref, ahead_ref, outer_ref, inner_ref, back_ref, weight_ref, links, field, lag, mortar, flat, line, sems):
+def position(relative, masks):
+    total = jnp.int32(0)
+    for n, mask in enumerate(masks):
+        total = total + jnp.where(jnp.bitwise_and(relative, mask) != 0, jnp.int32(1 << n), jnp.int32(0))
+    return total
+
+
+def routes(links, lines, mine, slots):
+    items = 2 * slots
+    patch, face = lines[0:2, :], lines[2:4, :]
+    hit = jnp.logical_and(patch == mine, jnp.broadcast_to(lines[4:5, :], patch.shape) > 0)
+    index = 2 * lax.broadcasted_iota(jnp.int32, patch.shape, 1) + lax.broadcasted_iota(jnp.int32, patch.shape, 0)
+    found = [jnp.sum(jnp.where(jnp.logical_and(hit, face == f), index, 0)) for f in range(4)]
+    one = lambda flag: jnp.where(flag, jnp.int32(1), jnp.int32(0))
+    once = lambda flags: jnp.minimum(functools.reduce(jnp.add, flags, jnp.int32(0)), 1)
+    owners = [lax.div(item, items) for item in found]
+    faces = []
+    for f in range(4):
+        mates = [(g, one(owners[g] == owners[f])) for g in range(4) if g != f]
+        first = once([mate for g, mate in mates if g < f])
+        faces.append((owners[f], first, 2 + once([mate * one(found[g] < found[f]) for g, mate in mates])))
+    base = mine * slots
+    patch = [links[t % 2, base + t // 2] for t in range(items)]
+    alive = [links[4, base + t // 2] > 0 for t in range(items)]
+    group = [jnp.where(alive[t], patch[t], -1 - t) for t in range(items)]
+    face = [links[2 + t % 2, base + t // 2] for t in range(items)]
+    lower = [[] for _ in range(items)]
+    earlier = [[] for _ in range(items)]
+    for t in range(items):
+        for u in range(t):
+            same = one(group[u] == group[t])
+            below = same * one(face[u] < face[t])
+            earlier[t].append(same)
+            lower[t].append(below)
+            lower[u].append(same - below)
+    own = [(patch[t], once(lower[t]), 2 + once(earlier[t])) for t in range(items)]
+    return faces, own
+
+
+def place(block, lane):
+    wide = jnp.concatenate([block, jnp.zeros((PAD, WIN - PAD), f32)], axis=1)
+    return pltpu.roll(wide, lane * PAD, axis=1)
+
+
+def prep_kernel(masks, links_hbm, field_hbm, lag_hbm, mortar_hbm, spread_hbm, ahead_hbm, outer_hbm, inner_hbm, back_hbm, weight_hbm, own_ref, wide_ref, sides_ref, route_ref, spread_ref, ahead_ref, outer_ref, inner_ref, back_ref, weight_ref, links, lines, field, lag, mortar, flat, line, sems):
     copies = start_all(
         [
             (field_hbm, field),
             (lag_hbm, lag),
             (links_hbm, links),
+            (links_hbm, lines),
             (mortar_hbm, mortar),
             (spread_hbm, spread_ref),
             (ahead_hbm, ahead_ref),
@@ -392,12 +448,16 @@
         sems,
     )
     slots = lag.shape[0]
+    items = 2 * slots
+    mine = lax.axis_index("patch")
     own_ref[...] = jnp.zeros(own_ref.shape, f32)
     line[...] = jnp.zeros(line.shape, f32)
+    sides_ref[...] = jnp.zeros(sides_ref.shape, f32)
     group, rows, fold = layers()
     same = rows == group
-    for copy in copies[:4]:
+    for copy in copies[:5]:
         copy.wait()
+    faces, own = routes(links, lines[...], mine, slots)
     load_flat(flat, field)
     for s in range(slots):
         line[s : s + 1, : BASIS * BASIS] = lag[s, 0]
@@ -412,104 +472,102 @@
     for x in spreads:
         parts.extend(split(x))
     squares = halves_sum(dot_nt(jnp.concatenate(parts, axis=0), fold), 4 + slots)
-    base = lax.axis_index("patch") * slots
-    halfway = []
+    base = mine * slots
     for s in range(slots):
         for side in range(2):
-            left = masked(mortar[s, side, :, 0, :], links[4, base + s])
-            halfway.append(dot_split(left, squares[s][:BASIS, :BASIS], ((0,), (0,))))
-    for s in range(slots):
-        for side in range(2):
-            right = masked(mortar[s, side, :, 1, :], links[5, base + s])
-            both = dot_split(halfway[2 * s + side], right, ((1,), (0,)))
-            item = 2 * s + side
-            at = (item % 4) * PAD
-            own_ref[1 + item // 4, :BASIS, at : at + BASIS] = both if side == 0 else -both
-    for f in range(4):
-        own_ref[0, :, f * PAD : (f + 1) * PAD] = squares[slots + f]
-    copies[4].wait()
+            for d in range(2):
+                sides_ref[2 * s + side, d, :BASIS, :BASIS] = masked(mortar[s, side, :, d, :], links[4 + d, base + s])
+    halfway = [dot_split(sides_ref[t, 0], squares[t // 2], ((0,), (0,))) for t in range(items)]
+    copies[5].wait()
     (wide,) = expand([flat[...]], spread_ref[...])
     wide_ref[...] = wide
-    for copy in copies[5:]:
+    for f in range(4):
+        patch, first, second = faces[f]
+        row = jnp.bitwise_xor(mine, patch)
+        own_ref[row] = own_ref[row] + place(squares[slots + f], first)
+    for t in range(items):
+        both = dot_split(halfway[t], sides_ref[t, 1], ((1,), (0,)))
+        patch, first, second = own[t]
+        row = jnp.bitwise_xor(mine, patch)
+        own_ref[row] = own_ref[row] + place(both if t % 2 == 0 else -both, second)
+    entries = []
+    for patch, first, second in faces:
+        entries += [position(jnp.bitwise_xor(mine, patch), masks), second]
+    for patch, first, second in own:
+        entries += [position(jnp.bitwise_xor(mine, patch), masks), first]
+    lane = lax.broadcasted_iota(jnp.int32, route_ref.shape, 1)
+    table = jnp.zeros(route_ref.shape, jnp.int32)
+    for n, entry in enumerate(entries):
+        table = jnp.where(lane == n, entry, table)
+    route_ref[...] = table
+    for copy in copies[6:]:
         copy.wait()
 
 
-def position(mine, other, masks):
-    differ = jnp.bitwise_xor(mine, other)
-    total = jnp.int32(0)
-    for n, mask in enumerate(masks):
-        total = total + jnp.where(jnp.bitwise_and(differ, mask) != 0, jnp.int32(1 << n), jnp.int32(0))
-    return total
-
-
-def final_kernel(masks, links_hbm, mortar_hbm, *refs):
-    rounds = len(masks)
-    part_refs = refs[: rounds + 1]
-    inner_ref, out_ref, jump_ref, buf, links, mortar, found, sems = refs[rounds + 1 :]
-    copies = start_all([(links_hbm, links), (mortar_hbm, mortar)], sems)
-    slots = mortar.shape[0]
-    mine = lax.axis_index("patch")
-    table = links.shape[1]
-    buf[0] = part_refs[0][...]
-    for n in range(rounds):
-        buf[(1 << n) : (2 << n)] = part_refs[n + 1][...].reshape((1 << n,) + buf.shape[1:])
+def final_kernel(groups, route_vmem, sides_ref, kept_ref, other_ref, stiff_a, stiff_b, volume_ref, wides_ref, spread_ref, ahead_ref, outer_ref, inner_ref, back_ref, weight_ref, out_ref, jump_ref, buf, mid_h, mid_l, prod, heads, route, sems):
+    copies = start_all([(route_vmem, route)], sems)
+    items = sides_ref.shape[0]
+    slots = items // 2
+    half = kept_ref.shape[0]
+    buf[:half] = kept_ref[...]
+    buf[half:] = other_ref[...]
     group, rows, fold = layers()
     same = rows == group
-    for f in range(5):
-        found[f] = 0
-    for copy in copies:
-        copy.wait()
-
-    def look(t, carry):
-        for side in range(2):
-            hit = jnp.logical_and(links[side, t] == mine, links[4, t] > 0)
-            found[jnp.where(hit, links[2 + side, t], 4)] = 2 * t + side
-        return carry
-
-    def pick(owner, plane, lane):
-        block = buf[position(mine, owner, masks), plane]
-        return pltpu.roll(block, lax.rem(WIN - lane * PAD, WIN), axis=1)[:, :PAD]
-
-    base = mine * slots
+    squares = []
     halfway = []
-    for s in range(slots):
-        for side in range(2):
-            trace = pick(links[side, base + s], 0, links[2 + side, base + s])
-            left = masked(mortar[s, side, :, 0, :], links[4, base + s])
-            halfway.append(dot_split(left, trace[:BASIS, :BASIS], ((1,), (0,))))
-    jumps = []
-    for s in range(slots):
-        total = None
-        for side in range(2):
-            right = masked(mortar[s, side, :, 1, :], links[5, base + s])
-            both = dot_split(halfway[2 * s + side], right, ((1,), (1,)))
-            total = both if total is None else total - both
-        jumps.append(jnp.pad(total, ((0, PAD - BASIS), (0, PAD - BASIS))))
-    if table <= 64:
-        for t in range(table):
-            look(t, 0)
-    else:
-        lax.fori_loop(0, table, look, 0, unroll=8)
-    squares = []
-    for f in range(4):
-        item = found[f]
-        owner = lax.div(item, 2 * slots)
-        item = lax.rem(item, 2 * slots)
-        squares.append(pick(owner, 1 + lax.div(item, 4), lax.rem(item, 4)))
-    parts = []
-    for x in squares + jumps:
-        parts.extend(split(x))
-    lines = halves_sum(dot(jnp.concatenate(parts, axis=0), fold), 4 + slots)
-    out = inner_ref[...]
-    low_row = jnp.sum(jnp.where(same, lines[0], 0.0), axis=0, keepdims=True)
-    high_row = jnp.sum(jnp.where(same, lines[1], 0.0), axis=0, keepdims=True)
-    out = out + jnp.where(rows == 0, low_row, 0.0) + jnp.where(rows == BASIS - 1, high_row, 0.0)
-    out = out + jnp.where(group == 0, lines[2], 0.0) + jnp.where(group == BASIS - 1, lines[3], 0.0)
+    both = []
+
+    def pick(n):
+        block = buf[route[0, 2 * n]]
+        return pltpu.roll(block, lax.rem(WIN - route[0, 2 * n + 1] * PAD, WIN), axis=1)[:, :PAD]
+
+    def start():
+        copies[0].wait()
+        halfway.extend(dot_split(sides_ref[t, 0], pick(4 + t), ((1,), (0,))) for t in range(items))
+        squares.extend(pick(f) for f in range(4))
+
+    def go_on():
+        both.extend(dot_split(halfway[t], sides_ref[t, 1], ((1,), (1,))) for t in range(items))
+
+    def end():
+        for s in range(slots):
+            squares.append(both[2 * s] - both[2 * s + 1])
+        parts = []
+        for x in squares:
+            parts.extend(split(x))
+        lines = halves_sum(dot(jnp.concatenate(parts, axis=0), fold), 4 + slots)
+        for s in range(slots):
+            row = jnp.sum(jnp.where(same, lines[4 + s], 0.0), axis=0, keepdims=True)
+            jump_ref[s, 0] = row[:, : BASIS * BASIS]
+        low_row = jnp.sum(jnp.where(same, lines[0], 0.0), axis=0, keepdims=True)
+        high_row = jnp.sum(jnp.where(same, lines[1], 0.0), axis=0, keepdims=True)
+        both.append(
+            jnp.where(rows == 0, low_row, 0.0)
+            + jnp.where(rows == BASIS - 1, high_row, 0.0)
+            + jnp.where(group == 0, lines[2], 0.0)
+            + jnp.where(group == BASIS - 1, lines[3], 0.0)
+        )
+
+    tables = volume_tables(outer_ref, inner_ref, back_ref)
+    volume = volume_groups(
+        groups,
+        [wides_ref[n] for n in range(3)],
+        ahead_ref,
+        tables,
+        weight_ref,
+        mid_h,
+        mid_l,
+        prod,
+        heads,
+        {0: start, 1: go_on, 2: end},
+    )
+    is_pressure = lax.axis_index("sub") == FIELDS - 1
+    factor = jnp.where(is_pressure, -stabilize, 1.0).astype(f32)
+    total = factor * (stiff_a[...] + stiff_b[...]) - (volume_ref[...] + volume)
+    out = dot_nt(jnp.concatenate(split(total), axis=0), spread_ref[...])
+    out = out[:PAD] + out[PAD:] + both[-1]
     for i in range(BASIS):
         out_ref[i] = out[i : i + 1, : BASIS * BASIS]
-    for s in range(slots):
-        row = jnp.sum(jnp.where(same, lines[4 + s], 0.0), axis=0, keepdims=True)
-        jump_ref[s, 0] = row[:, : BASIS * BASIS]
 
 
 def vmem():
@@ -550,47 +608,72 @@
     )(wide, *tables[1:], weight, *in_hbm(following))
 
 
-def volume_call(near, far, tables, weight, stiff_a, stiff_b):
+def volume_scratch(count):
+    return [
+        pltpu.VMEM((count * GROUP_ROWS, 2 * SPAN), bf16),
+        pltpu.VMEM((count * GROUP_ROWS, 2 * SPAN), bf16),
+        pltpu.VMEM((2, 2 * QUAD, 2 * SPAN), bf16),
+        pltpu.VMEM((2 * count * GROUP_ROWS, SPAN), bf16),
+    ]
+
+
+def volume_call(groups, near, far, tables, weight):
     return pl.pallas_call(
-        volume_kernel,
-        out_shape=jax.ShapeDtypeStruct((PAD, FLAT), f32),
-        in_specs=[vmem()] * 10,
-        out_specs=vmem(),
-        scratch_shapes=[
-            pltpu.VMEM((3, PAD, FLAT), f32),
-            pltpu.VMEM((ELEMS * PAD, 2 * SPAN), bf16),
-            pltpu.VMEM((ELEMS * PAD, 2 * SPAN), bf16),
-            pltpu.VMEM((2, 2 * QUAD, 2 * SPAN), bf16),
-            pltpu.VMEM((2 * ELEMS * PAD, SPAN), bf16),
-        ],
+        functools.partial(volume_kernel, groups),
+        out_shape=(jax.ShapeDtypeStruct((PAD, WIDE), f32), jax.ShapeDtypeStruct((3, PAD, WIDE), f32)),
+        in_specs=[vmem()] * 8,
+        out_specs=(vmem(), vmem()),
+        scratch_shapes=[pltpu.VMEM((3, PAD, FLAT), f32)] + volume_scratch(len(groups)),
         compiler_params=params,
-    )(near, far, *tables, weight, stiff_a, stiff_b)
-
-
-def prep_call(links, field, lagrange, mortar, tables, stiff_weight, planes):
+    )(near, far, *tables, weight)
+
+
+def prep_call(masks, links, field, lagrange, mortar, tables, stiff_weight):
+    slots = mortar.shape[0]
+    patches = 1 << len(masks)
     return pl.pallas_call(
-        prep_kernel,
+        functools.partial(prep_kernel, masks),
         out_shape=(
-            jax.ShapeDtypeStruct((planes, PAD, WIN), f32),
+            jax.ShapeDtypeStruct((patches, PAD, WIN), f32),
             jax.ShapeDtypeStruct((PAD, WIDE), f32),
+            jax.ShapeDtypeStruct((2 * slots, 2, PAD, PAD), f32),
+            jax.ShapeDtypeStruct((1, WIN), jnp.int32),
             *(jax.ShapeDtypeStruct(t.shape, bf16) for t in tables),
             jax.ShapeDtypeStruct((QUAD, halfspan), f32),
         ),
         in_specs=[anywhere()] * 10,
-        out_specs=(vmem(),) * 8,
+        out_specs=(vmem(),) * 10,
         scratch_shapes=[
             pltpu.SMEM(links.shape, jnp.int32),
+            pltpu.VMEM(links.shape, jnp.int32),
             pltpu.VMEM(field.shape, f32),
             pltpu.VMEM(lagrange.shape, f32),
             pltpu.VMEM(mortar.shape, f32),
             pltpu.VMEM((PAD, FLAT), f32),
             pltpu.VMEM((8, FLAT), f32),
-            pltpu.SemaphoreType.DMA((10,)),
+            pltpu.SemaphoreType.DMA((11,)),
         ],
         compiler_params=params,
     )(*in_hbm(links, field, lagrange, mortar, *tables, stiff_weight))
 
 
+def final_call(groups, route, sides, kept, other, stiff_a, stiff_b, volume, wides, tables, weight, field):
+    slots = sides.shape[0] // 2
+    return pl.pallas_call(
+        functools.partial(final_kernel, groups),
+        out_shape=(
+            jax.ShapeDtypeStruct(field.shape, f32),
+            jax.ShapeDtypeStruct((slots, 1, 1, BASIS * BASIS), f32),
+        ),
+        in_specs=[vmem()] * 14,
+        out_specs=(vmem(), vmem()),
+        scratch_shapes=[pltpu.VMEM((2 * kept.shape[0], PAD, WIN), f32)]
+        + volume_scratch(len(groups))
+        + [pltpu.SMEM((1, WIN), jnp.int32), pltpu.SemaphoreType.DMA((1,))],
+        compiler_params=params,
+    )(route, sides, kept, other, stiff_a, stiff_b, volume, wides, *tables, weight)
+
+
 def swap(array, axis, mask):
     size = lax.axis_size(axis)
     return lax.ppermute(array, axis, [(n, n ^ mask) for n in range(size)])
@@ -603,50 +686,33 @@
 def per_device(state, stiff_weight, volume_weight, lagrange, mortar, links):
     tables = [jnp.asarray(constants()[name]) for name in ("spread", "ahead", "outer", "inner", "back")]
     patches = lax.axis_size("patch")
-    slots = mortar.shape[0]
-    planes = 1 + (2 * slots + 3) // 4
     masks = [1 << n for n in reversed(range(patches.bit_length() - 1))]
     field = jnp.transpose(state, (0, 1, 3, 2, 4))[0, 0]
     mortar = jnp.transpose(mortar, (0, 1, 3, 2, 4))
     links = links.T
 
     near = swap(field, "sub", 1)
-    own, wide, *tables, weight_a = prep_call(links, field, lagrange, mortar, tables, stiff_weight, planes)
+    own, wide, sides, route, *tables, weight_a = prep_call(masks, links, field, lagrange, mortar, tables, stiff_weight)
     far = swap(jnp.stack([field, near]), "sub", 2)
     first = GROUPS // 2
     stiff_a, weight_b = stiff_call(
         list(range(first)), (halfspan, ELEMS * SPAN - halfspan), wide, tables, weight_a, stiff_weight
     )
-    stiff_b, weight_c = stiff_call(
-        list(range(first, GROUPS)), (0, ELEMS * SPAN), wide, tables, weight_b, volume_weight
-    )
-    inner = volume_call(near, far, tables, weight_c, stiff_a, stiff_b)
+    stiff_b, weight_c = stiff_call(list(range(first, GROUPS)), (0, ELEMS * SPAN), wide, tables, weight_b, volume_weight)
+    volume, wides = volume_call(list(range(EARLY)), near, far, tables, weight_c)
     gates = [None, stiff_a, stiff_b]
-    parts = [own]
-    held = own
+    held = own[None]
     for n, mask in enumerate(masks):
         late = len(masks) - n
-        gate = gates[max(0, 3 - late)] if n > 0 else None
-        other = swap(held if gate is None else after(held, gate), "patch", mask)
-        parts.append(other)
-        held = jnp.concatenate([held, other], axis=0)
-    residual, constraint = pl.pallas_call(
-        functools.partial(final_kernel, masks),
-        out_shape=(
-            jax.ShapeDtypeStruct(field.shape, f32),
-            jax.ShapeDtypeStruct((slots, 1, 1, BASIS * BASIS), f32),
-        ),
-        in_specs=[anywhere(), anywhere()] + [vmem()] * (len(parts) + 1),
-        out_specs=(vmem(), vmem()),
-        scratch_shapes=[
-            pltpu.VMEM((patches, planes, PAD, WIN), f32),
-            pltpu.SMEM(links.shape, jnp.int32),
-            pltpu.VMEM(mortar.shape, f32),
-            pltpu.SMEM((8,), jnp.int32),
-            pltpu.SemaphoreType.DMA((2,)),
-        ],
-        compiler_params=params,
-    )(*in_hbm(links, mortar), *parts, inner)
+        gate = gates[max(0, 3 - late)]
+        half = held.shape[1] // 2
+        send = held[:, half:]
+        other = swap(send if gate is None else after(send, gate), "patch", mask)
+        kept = held[:, :half]
+        held = jnp.concatenate([kept, other], axis=0)
+    residual, constraint = final_call(
+        list(range(EARLY, GROUPS)), route, sides, kept[:, 0], other[:, 0], stiff_a, stiff_b, volume, wides, tables, weight_c, field
+    )
     return jnp.transpose(residual[None, None], (0, 1, 3, 2, 4)), constraint
 
 

time: 30 us -> 28.3 us (0.943)
  waiting for transfers between devices: 4.91 us -> 3.3 us
    ppermute x5, waiting for transfers between devices: 4.91 us -> 3.3 us  [swap(): return lax.ppermute(array, axis, [(n, n ^ mask) for n in range(size)])]
  transfers between devices with their start and end apart: 5 -> 5, of which waited for: 1 -> 2; matrix products, arithmetic and copies ran while one was open for 1% -> 1% of each run, Pallas kernels for 34% -> 31%
where the time goes in v2:
time: 28.3 us; the launch traced here: 28.2 us
  Pallas kernels  15 us (53%)
  starting transfers between devices  8.91 us (31%)
  waiting for transfers between devices  3.3 us (12%)
  between operations  0.71 us (3%)
    ppermute x5, starting transfers between devices, swap(): return lax.ppermute(array, axis, [(n, n ^ mask) for n in range(size)])  8.91 us
    pallas_call x2, Pallas kernels, stiff_call(): pl.pallas_call(functools.partial(stiff_kernel, groups, lanes), out_shape=...  6.13 us
    pallas_call x1, Pallas kernels, final_call(): pl.pallas_call(functools.partial(final_kernel, groups), out_shape=(jax.Sh...  3.55 us
    ppermute x5, waiting for transfers between devices, swap(): return lax.ppermute(array, axis, [(n, n ^ mask) for n in range(size)])  3.3 us
    pallas_call x1, Pallas kernels, prep_call(): pl.pallas_call(functools.partial(prep_kernel, masks), out_shape=(jax.Shap...  2.7 us
    pallas_call x1, Pallas kernels, volume_call(): pl.pallas_call(functools.partial(volume_kernel, groups), out_shape=(jax.S...  2.66 us
  transfers between devices with their start and end apart: 5, of which 2 were waited for; matrix products, arithmetic and copies ran while one was open for 1% of the time, Pallas kernels for 31%

profile of v2, /device:TPU:0, one launch (start us, length us, event | category | flops | bytes accessed | tf_op | source)
XLA Modules:
  0.0 28.2 jit_solution(8952286822702818833)
XLA Ops:
  0.6 0.0 copy-start
  0.6 2.7 %shard_map.122 = (f32[8,32,128]{2,1,0:T(8,128)S(1)}, f32[32,896]{1,0:T(8,128)S(1)}, f32[8,2,32,32]{3,2,1,0:T(8,128)S(1)}, s32[1,128]{1,0:T(1,128)S(1)}, bf16[768...) custom-call(s32[6,32]{1,0:T(8,128)} %bitcast.19, ...), custom_call_target="tpu_custom_call" | custom-call | tf_op jit(solution)/shard_map/pallas_call | solution.py:634
  3.4 4.1 %collective-permute-start = (f32[1,4,32,128]{3,2,0,1:T(8,128)S(1)}, f32[1,4,32,128]{3,2,0,1:T(8,128)S(1)}, u32[]{:S(2)}, u32[]{:S(2)}) collective-permute-start(f32[1,4,32,128]{3,2,0,1:T(8,128)S(1)} %get-tuple-element.48), channel_id=1, source_target_pairs={{0,16},{4,20},{8,24},{12,28},{16,0},{20,4},{24,8},{28,12},{1,17},{... | collective-permute-start | bytes 196616 | tf_op jit(solution)/shard_map/ppermute | solution.py:679
  7.5 0.0 copy-done
  7.5 0.0 collective-permute-start.3
  7.5 3.1 %shard_map.123 = (f32[32,896]{1,0:T(8,128)S(1)}, f32[96,4608]{1,0:T(8,128)S(1)}) custom-call(f32[32,896]{1,0:T(8,128)S(1)} %get-tuple-element.25.wide_ref, bf16[384,1152]{1,0:T(8,128)(2,1)S(1)} %get-tuple-element.26.ahead_ref, bf16[2,96,96]{2,1,0:T(8,128)(2,1)S(1)} %get-tuple-element.27.outer_ref, bf16[2,64,192]{2,1,0:T(8,128)(2,1)S(1)} %get-tuple-element.28.inner_ref, ...), custom_call_target="tpu_custom_call" | custom-call | tf_op jit(solution)/shard_map/pallas_call | solution.py:592
  10.6 3.1 %shard_map.124 = (f32[32,896]{1,0:T(8,128)S(1)}, f32[96,9216]{1,0:T(8,128)S(1)}) custom-call(f32[32,896]{1,0:T(8,128)S(1)} %get-tuple-element.25.wide_ref, bf16[384,1152]{1,0:T(8,128)(2,1)S(1)} %get-tuple-element.26.ahead_ref, bf16[2,96,96]{2,1,0:T(8,128)(2,1)S(1)} %get-tuple-element.27.outer_ref, bf16[2,64,192]{2,1,0:T(8,128)(2,1)S(1)} %get-tuple-element.28.inner_ref, ...), custom_call_target="tpu_custom_call" | custom-call | tf_op jit(solution)/shard_map/pallas_call | solution.py:592
  13.7 0.0 collective-permute-done
  13.7 1.6 %collective-permute-start.1 = (f32[2,2,32,128]{3,2,0,1:T(8,128)S(1)}, f32[2,2,32,128]{3,2,0,1:T(8,128)S(1)}, u32[]{:S(2)}, u32[]{:S(2)}) collective-permute-start(f32[2,2,32,128]{3,2,0,1:T(8,128)S(1)} %get-tuple-element.32), channel_id=1, source_target_pairs={{0,8},{4,12},{8,0},{12,4},{16,24},{20,28},{24,16},{28,20},{1,9},{5... | collective-permute-start | bytes 196616 | tf_op jit(solution)/shard_map/ppermute | solution.py:679
  15.3 0.0 collective-permute-done.3.near_ref
  15.3 0.1 pad_maximum_fusion
  15.5 1.6 %collective-permute-start.4 = (f32[2,27,1,729]{3,2,1,0:T(1,128)S(1)}, f32[2,27,1,729]{3,2,1,0:T(1,128)S(1)}, u32[]{:S(2)}, u32[]{:S(2)}) collective-permute-start(f32[2,27,1,729]{3,2,1,0:T(1,128)S(1)} %pad_maximum_fusion), channel_id=1, source_target_pairs={{0,2},{1,3},{2,0},{3,1},{4,6},{5,7},{6,4},{7,5},{8,10},{9,11},{10,... | collective-permute-start | bytes 472400 | tf_op jit(solution)/shard_map/ppermute | solution.py:679
  17.0 1.2 %collective-permute-done.1 = f32[2,2,32,128]{3,2,0,1:T(8,128)S(1)} collective-permute-done((f32[2,2,32,128]{3,2,0,1:T(8,128)S(1)}, f32[2,2,32,128]{3,2,0,1:T(8,128)S(1)}, u32[]{:S(2)}, u32[]{:S(2)}) %collective-permute-start.1) | collective-permute-done | bytes 65568 | tf_op jit(solution)/shard_map/ppermute | solution.py:679
  18.3 1.6 %collective-permute-start.2 = (f32[4,1,32,128]{3,2,0,1:T(8,128)S(1)}, f32[4,1,32,128]{3,2,0,1:T(8,128)S(1)}, u32[]{:S(2)}, u32[]{:S(2)}) collective-permute-start(f32[4,1,32,128]{3,2,0,1:T(8,128)S(1)} %get-tuple-element.35), channel_id=1, source_target_pairs={{0,4},{4,0},{8,12},{12,8},{16,20},{20,16},{24,28},{28,24},{1,5},{5... | collective-permute-start | bytes 196616 | tf_op jit(solution)/shard_map/ppermute | solution.py:679
  19.9 2.1 %collective-permute-done.4.far_ref = f32[2,27,1,729]{3,2,1,0:T(1,128)S(1)} collective-permute-done((f32[2,27,1,729]{3,2,1,0:T(1,128)S(1)}, f32[2,27,1,729]{3,2,1,0:T(1,128)S(1)}, u32[]{:S(2)}, u32[]{:S(2)}) %collective-permute-start.4) | collective-permute-done | bytes 157496 | tf_op jit(solution)/shard_map/ppermute | solution.py:679
  21.9 2.7 %shard_map.125 = (f32[32,896]{1,0:T(8,128)S(1)}, f32[3,32,896]{2,1,0:T(8,128)S(1)}) custom-call(f32[27,1,729]{2,1,0:T(1,128)S(1)} %collective-permute-done.3.near_ref, f32[2,27,1,729]{3,2,1,0:T(1,128)S(1)} %collective-permute-done.4.far_ref, bf16[768,896]{1,0:T(8,128)(2,1)S(1)} %get-tuple-element.36.spread_ref, ...), custom_call_target="tpu_custom_call" | custom-call | tf_op jit(solution)/shard_map/pallas_call | solution.py:621
  24.6 0.0 collective-permute-done.2
  24.6 3.5 %shard_map.126 = (f32[27,1,729]{2,1,0:T(1,128)}, f32[4,1,1,729]{3,2,1,0:T(1,128)}) custom-call(s32[1,128]{1,0:T(1,128)S(1)} %get-tuple-element.22.route_vmem, f32[8,2,32,32]{3,2,1,0:T(8,128)S(1)} %get-tuple-element.23.sides_ref, f32[4,32,128]{2,1,0:T(8,128)S(1)} %get-tuple-element.45.kept_ref, f32[4,32,128]{2,1,0:T(8,128)S(1)} %bitcast.14, ...), custom_call_target="tpu_custom_call" | custom-call | tf_op jit(solution)/shard_map/pallas_call | solution.py:662
  (3 shorter events, 0.0 us)
Async XLA Ops:
  0.6 6.9 %copy-start = (f32[1,1,1,27,729]{4,2,3,1,0:T(1,128)S(1)}, f32[1,1,1,27,729]{4,2,3,1,0:T(1,128)}, u32[]{:S(2)}) copy-start(f32[1,1,1,27,729]{4,2,3,1,0:T(1,128)} %param.11) | copy-start | bytes 236200
  3.4 10.3 %collective-permute-start = (f32[1,4,32,128]{3,2,0,1:T(8,128)S(1)}, f32[1,4,32,128]{3,2,0,1:T(8,128)S(1)}, u32[]{:S(2)}, u32[]{:S(2)}) collective-permute-start(f32[1,4,32,128]{3,2,0,1:T(8,128)S(1)} %get-tuple-element.48), channel_id=1, source_target_pairs={{0,16},{4,20},{8,24},{12,28},{16,0},{20,4},{24,8},{28,12},{1,17},{... | collective-permute-start | bytes 196616 | tf_op jit(solution)/shard_map/ppermute | solution.py:679
  7.5 7.8 %collective-permute-start.3 = (f32[27,1,729]{2,1,0:T(1,128)S(1)}, f32[27,1,729]{2,1,0:T(1,128)S(1)}, u32[]{:S(2)}, u32[]{:S(2)}) collective-permute-start(f32[27,1,729]{2,1,0:T(1,128)S(1)} %bitcast.16), channel_id=1, source_target_pairs={{0,1},{1,0},{2,3},{3,2},{4,5},{5,4},{6,7},{7,6},{8,9},{9,8},{10,11... | collective-permute-start | bytes 236204 | tf_op jit(solution)/shard_map/ppermute | solution.py:679
  13.7 4.6 %collective-permute-start.1 = (f32[2,2,32,128]{3,2,0,1:T(8,128)S(1)}, f32[2,2,32,128]{3,2,0,1:T(8,128)S(1)}, u32[]{:S(2)}, u32[]{:S(2)}) collective-permute-start(f32[2,2,32,128]{3,2,0,1:T(8,128)S(1)} %get-tuple-element.32), channel_id=1, source_target_pairs={{0,8},{4,12},{8,0},{12,4},{16,24},{20,28},{24,16},{28,20},{1,9},{5... | collective-permute-start | bytes 196616 | tf_op jit(solution)/shard_map/ppermute | solution.py:679
  15.5 6.4 %collective-permute-start.4 = (f32[2,27,1,729]{3,2,1,0:T(1,128)S(1)}, f32[2,27,1,729]{3,2,1,0:T(1,128)S(1)}, u32[]{:S(2)}, u32[]{:S(2)}) collective-permute-start(f32[2,27,1,729]{3,2,1,0:T(1,128)S(1)} %pad_maximum_fusion), channel_id=1, source_target_pairs={{0,2},{1,3},{2,0},{3,1},{4,6},{5,7},{6,4},{7,5},{8,10},{9,11},{10,... | collective-permute-start | bytes 472400 | tf_op jit(solution)/shard_map/ppermute | solution.py:679
  18.3 6.3 %collective-permute-start.2 = (f32[4,1,32,128]{3,2,0,1:T(8,128)S(1)}, f32[4,1,32,128]{3,2,0,1:T(8,128)S(1)}, u32[]{:S(2)}, u32[]{:S(2)}) collective-permute-start(f32[4,1,32,128]{3,2,0,1:T(8,128)S(1)} %get-tuple-element.35), channel_id=1, source_target_pairs={{0,4},{4,0},{8,12},{12,8},{16,20},{20,16},{24,28},{28,24},{1,5},{5... | collective-permute-start | bytes 196616 | tf_op jit(solution)/shard_map/ppermute | solution.py:679

commit v3 on v2

--- a/solution.py
+++ b/solution.py
@@ -24,6 +24,8 @@
 WIDE = (GROUPS + 1) * WIN
 FLAT = 768
 GROUP_ROWS = 4 * PAD
+BLOCK = 256
+BLOCK_WIDE = 384
 
 stabilize = 0.25
 f32 = jnp.float32
@@ -137,13 +139,17 @@
     for k in range(BASIS):
         spread[:, k, :BASIS, k] = change.T
     spread = padded(spread.reshape(BASIS * BASIS, WIDE), FLAT, WIDE)
+    blocks = [
+        spread[n * BLOCK : (n + 1) * BLOCK, n * BLOCK : n * BLOCK + BLOCK_WIDE] for n in range(FLAT // BLOCK)
+    ]
+    assert sum(np.count_nonzero(block) for block in blocks) == np.count_nonzero(spread)
     as16 = lambda a: a.astype(np.dtype(bf16))
     return dict(
         ahead=as16(ahead3),
         back=as16(back2),
         outer=as16(np.stack([left3(slope), left3(value)])),
         inner=as16(np.stack([left4(slope_w), left4(value_w)])),
-        spread=as16(spread),
+        spread=as16(np.stack(blocks)),
     )
 
 
@@ -160,12 +166,28 @@
     return lax.dot_general(a, b, (((1,), (1,)), ((), ())), preferred_element_type=f32)
 
 
-def expand(fields, spread):
+def expand(fields, spread_ref):
     parts = []
     for field in fields:
         parts.extend(split(field))
-    out = dot(jnp.concatenate(parts, axis=0), spread)
+    rows = jnp.concatenate(parts, axis=0)
+    out = None
+    for n in range(FLAT // BLOCK):
+        piece = dot(rows[:, n * BLOCK : (n + 1) * BLOCK], spread_ref[n])
+        left, right = n * BLOCK, WIDE - n * BLOCK - BLOCK_WIDE
+        sides = [jnp.zeros((rows.shape[0], width), f32) for width in (left, right)]
+        pieces = ([sides[0]] if left else []) + [piece] + ([sides[1]] if right else [])
+        piece = jnp.concatenate(pieces, axis=1)
+        out = piece if out is None else out + piece
     return halves_sum(out, len(fields))
+
+
+def contract(wide, spread_ref):
+    rows = jnp.concatenate(split(wide), axis=0)
+    out = [
+        dot_nt(rows[:, n * BLOCK : n * BLOCK + BLOCK_WIDE], spread_ref[n]) for n in range(FLAT // BLOCK)
+    ]
+    return halves_sum(jnp.concatenate(out, axis=1), 1)[0]
 
 
 def halves_sum(out, count):
@@ -358,7 +380,7 @@
         jnp.where(is_pressure, flat[1], zero),
         jnp.where(is_pressure, flat[0], zero),
     ]
-    wides = expand(fields, spread_ref[...])
+    wides = expand(fields, spread_ref)
     for n in range(3):
         wides_ref[n] = wides[n]
     tables = volume_tables(outer_ref, inner_ref, back_ref)
@@ -479,7 +501,7 @@
                 sides_ref[2 * s + side, d, :BASIS, :BASIS] = masked(mortar[s, side, :, d, :], links[4 + d, base + s])
     halfway = [dot_split(sides_ref[t, 0], squares[t // 2], ((0,), (0,))) for t in range(items)]
     copies[5].wait()
-    (wide,) = expand([flat[...]], spread_ref[...])
+    (wide,) = expand([flat[...]], spread_ref)
     wide_ref[...] = wide
     for f in range(4):
         patch, first, second = faces[f]
@@ -564,8 +586,7 @@
     is_pressure = lax.axis_index("sub") == FIELDS - 1
     factor = jnp.where(is_pressure, -stabilize, 1.0).astype(f32)
     total = factor * (stiff_a[...] + stiff_b[...]) - (volume_ref[...] + volume)
-    out = dot_nt(jnp.concatenate(split(total), axis=0), spread_ref[...])
-    out = out[:PAD] + out[PAD:] + both[-1]
+    out = contract(total, spread_ref) + both[-1]
     for i in range(BASIS):
         out_ref[i] = out[i : i + 1, : BASIS * BASIS]
 

time: 28.3 us -> 27.6 us (0.975)
  Pallas kernels: 15 us -> 14.3 us
    pallas_call x1, Pallas kernels: 3.55 us -> 3.05 us  [final_call(): pl.pallas_call(functools.partial(final_kernel, groups), out_shape=(jax.Sh...]
  transfers between devices with their start and end apart: 5 -> 5, of which waited for: 2 -> 2; matrix products, arithmetic and copies ran while one was open for 1% -> 1% of each run, Pallas kernels for 31% -> 32%
where the time goes in v3:
time: 27.6 us; the launch traced here: 27.4 us
  Pallas kernels  14.3 us (52%)
  starting transfers between devices  8.91 us (32%)
  waiting for transfers between devices  3.29 us (12%)
  between operations  0.71 us (3%)
    ppermute x5, starting transfers between devices, swap(): return lax.ppermute(array, axis, [(n, n ^ mask) for n in range(size)])  8.91 us
    pallas_call x2, Pallas kernels, stiff_call(): pl.pallas_call(functools.partial(stiff_kernel, groups, lanes), out_shape=...  6.2 us
    ppermute x5, waiting for transfers between devices, swap(): return lax.ppermute(array, axis, [(n, n ^ mask) for n in range(size)])  3.29 us
    pallas_call x1, Pallas kernels, final_call(): pl.pallas_call(functools.partial(final_kernel, groups), out_shape=(jax.Sh...  3.05 us
    pallas_call x1, Pallas kernels, volume_call(): pl.pallas_call(functools.partial(volume_kernel, groups), out_shape=(jax.S...  2.63 us
    pallas_call x1, Pallas kernels, prep_call(): pl.pallas_call(functools.partial(prep_kernel, masks), out_shape=(jax.Shap...  2.47 us
  transfers between devices with their start and end apart: 5, of which 2 were waited for; matrix products, arithmetic and copies ran while one was open for 1% of the time, Pallas kernels for 32%

profile of v3, /device:TPU:0, one launch (start us, length us, event | category | flops | bytes accessed | tf_op | source)
XLA Modules:
  0.0 27.4 jit_solution(9536092774856320622)
XLA Ops:
  0.6 0.0 copy-start
  0.6 2.5 %shard_map.122 = (f32[8,32,128]{2,1,0:T(8,128)S(1)}, f32[32,896]{1,0:T(8,128)S(1)}, f32[8,2,32,32]{3,2,1,0:T(8,128)S(1)}, s32[1,128]{1,0:T(1,128)S(1)}, bf16[3,2...) custom-call(s32[6,32]{1,0:T(8,128)} %bitcast.19, ...), custom_call_target="tpu_custom_call" | custom-call | tf_op jit(solution)/shard_map/pallas_call | solution.py:655
  3.1 4.1 %collective-permute-start = (f32[1,4,32,128]{3,2,0,1:T(8,128)S(1)}, f32[1,4,32,128]{3,2,0,1:T(8,128)S(1)}, u32[]{:S(2)}, u32[]{:S(2)}) collective-permute-start(f32[1,4,32,128]{3,2,0,1:T(8,128)S(1)} %get-tuple-element.48), channel_id=1, source_target_pairs={{0,16},{4,20},{8,24},{12,28},{16,0},{20,4},{24,8},{28,12},{1,17},{... | collective-permute-start | bytes 196616 | tf_op jit(solution)/shard_map/ppermute | solution.py:700
  7.3 0.0 copy-done
  7.3 0.0 collective-permute-start.3
  7.3 3.1 %shard_map.123 = (f32[32,896]{1,0:T(8,128)S(1)}, f32[96,4608]{1,0:T(8,128)S(1)}) custom-call(f32[32,896]{1,0:T(8,128)S(1)} %get-tuple-element.25.wide_ref, bf16[384,1152]{1,0:T(8,128)(2,1)S(1)} %get-tuple-element.26.ahead_ref, bf16[2,96,96]{2,1,0:T(8,128)(2,1)S(1)} %get-tuple-element.27.outer_ref, bf16[2,64,192]{2,1,0:T(8,128)(2,1)S(1)} %get-tuple-element.28.inner_ref, ...), custom_call_target="tpu_custom_call" | custom-call | tf_op jit(solution)/shard_map/pallas_call | solution.py:613
  10.4 3.1 %shard_map.124 = (f32[32,896]{1,0:T(8,128)S(1)}, f32[96,9216]{1,0:T(8,128)S(1)}) custom-call(f32[32,896]{1,0:T(8,128)S(1)} %get-tuple-element.25.wide_ref, bf16[384,1152]{1,0:T(8,128)(2,1)S(1)} %get-tuple-element.26.ahead_ref, bf16[2,96,96]{2,1,0:T(8,128)(2,1)S(1)} %get-tuple-element.27.outer_ref, bf16[2,64,192]{2,1,0:T(8,128)(2,1)S(1)} %get-tuple-element.28.inner_ref, ...), custom_call_target="tpu_custom_call" | custom-call | tf_op jit(solution)/shard_map/pallas_call | solution.py:613
  13.5 0.0 collective-permute-done
  13.5 1.6 %collective-permute-start.1 = (f32[2,2,32,128]{3,2,0,1:T(8,128)S(1)}, f32[2,2,32,128]{3,2,0,1:T(8,128)S(1)}, u32[]{:S(2)}, u32[]{:S(2)}) collective-permute-start(f32[2,2,32,128]{3,2,0,1:T(8,128)S(1)} %get-tuple-element.32), channel_id=1, source_target_pairs={{0,8},{4,12},{8,0},{12,4},{16,24},{20,28},{24,16},{28,20},{1,9},{5... | collective-permute-start | bytes 196616 | tf_op jit(solution)/shard_map/ppermute | solution.py:700
  15.2 0.0 collective-permute-done.3.near_ref
  15.2 0.1 pad_maximum_fusion
  15.3 1.6 %collective-permute-start.4 = (f32[2,27,1,729]{3,2,1,0:T(1,128)S(1)}, f32[2,27,1,729]{3,2,1,0:T(1,128)S(1)}, u32[]{:S(2)}, u32[]{:S(2)}) collective-permute-start(f32[2,27,1,729]{3,2,1,0:T(1,128)S(1)} %pad_maximum_fusion), channel_id=1, source_target_pairs={{0,2},{1,3},{2,0},{3,1},{4,6},{5,7},{6,4},{7,5},{8,10},{9,11},{10,... | collective-permute-start | bytes 472400 | tf_op jit(solution)/shard_map/ppermute | solution.py:700
  16.9 1.2 %collective-permute-done.1 = f32[2,2,32,128]{3,2,0,1:T(8,128)S(1)} collective-permute-done((f32[2,2,32,128]{3,2,0,1:T(8,128)S(1)}, f32[2,2,32,128]{3,2,0,1:T(8,128)S(1)}, u32[]{:S(2)}, u32[]{:S(2)}) %collective-permute-start.1) | collective-permute-done | bytes 65568 | tf_op jit(solution)/shard_map/ppermute | solution.py:700
  18.1 1.6 %collective-permute-start.2 = (f32[4,1,32,128]{3,2,0,1:T(8,128)S(1)}, f32[4,1,32,128]{3,2,0,1:T(8,128)S(1)}, u32[]{:S(2)}, u32[]{:S(2)}) collective-permute-start(f32[4,1,32,128]{3,2,0,1:T(8,128)S(1)} %get-tuple-element.35), channel_id=1, source_target_pairs={{0,4},{4,0},{8,12},{12,8},{16,20},{20,16},{24,28},{28,24},{1,5},{5... | collective-permute-start | bytes 196616 | tf_op jit(solution)/shard_map/ppermute | solution.py:700
  19.7 2.1 %collective-permute-done.4.far_ref = f32[2,27,1,729]{3,2,1,0:T(1,128)S(1)} collective-permute-done((f32[2,27,1,729]{3,2,1,0:T(1,128)S(1)}, f32[2,27,1,729]{3,2,1,0:T(1,128)S(1)}, u32[]{:S(2)}, u32[]{:S(2)}) %collective-permute-start.4) | collective-permute-done | bytes 157496 | tf_op jit(solution)/shard_map/ppermute | solution.py:700
  21.7 2.6 %shard_map.125 = (f32[32,896]{1,0:T(8,128)S(1)}, f32[3,32,896]{2,1,0:T(8,128)S(1)}) custom-call(f32[27,1,729]{2,1,0:T(1,128)S(1)} %collective-permute-done.3.near_ref, f32[2,27,1,729]{3,2,1,0:T(1,128)S(1)} %collective-permute-done.4.far_ref, bf16[3,256,384]{2,1,0:T(8,128)(2,1)S(1)} %get-tuple-element.36.spread_ref, ...), custom_call_target="tpu_custom_call" | custom-call | tf_op jit(solution)/shard_map/pallas_call | solution.py:642
  24.4 0.0 collective-permute-done.2
  24.4 3.1 %shard_map.126 = (f32[27,1,729]{2,1,0:T(1,128)}, f32[4,1,1,729]{3,2,1,0:T(1,128)}) custom-call(s32[1,128]{1,0:T(1,128)S(1)} %get-tuple-element.22.route_vmem, f32[8,2,32,32]{3,2,1,0:T(8,128)S(1)} %get-tuple-element.23.sides_ref, f32[4,32,128]{2,1,0:T(8,128)S(1)} %get-tuple-element.45.kept_ref, f32[4,32,128]{2,1,0:T(8,128)S(1)} %bitcast.14, ...), custom_call_target="tpu_custom_call" | custom-call | tf_op jit(solution)/shard_map/pallas_call | solution.py:683
  (3 shorter events, 0.0 us)
Async XLA Ops:
  0.6 6.6 %copy-start = (f32[1,1,1,27,729]{4,2,3,1,0:T(1,128)S(1)}, f32[1,1,1,27,729]{4,2,3,1,0:T(1,128)}, u32[]{:S(2)}) copy-start(f32[1,1,1,27,729]{4,2,3,1,0:T(1,128)} %param.11) | copy-start | bytes 236200
  3.1 10.4 %collective-permute-start = (f32[1,4,32,128]{3,2,0,1:T(8,128)S(1)}, f32[1,4,32,128]{3,2,0,1:T(8,128)S(1)}, u32[]{:S(2)}, u32[]{:S(2)}) collective-permute-start(f32[1,4,32,128]{3,2,0,1:T(8,128)S(1)} %get-tuple-element.48), channel_id=1, source_target_pairs={{0,16},{4,20},{8,24},{12,28},{16,0},{20,4},{24,8},{28,12},{1,17},{... | collective-permute-start | bytes 196616 | tf_op jit(solution)/shard_map/ppermute | solution.py:700
  7.3 7.9 %collective-permute-start.3 = (f32[27,1,729]{2,1,0:T(1,128)S(1)}, f32[27,1,729]{2,1,0:T(1,128)S(1)}, u32[]{:S(2)}, u32[]{:S(2)}) collective-permute-start(f32[27,1,729]{2,1,0:T(1,128)S(1)} %bitcast.16), channel_id=1, source_target_pairs={{0,1},{1,0},{2,3},{3,2},{4,5},{5,4},{6,7},{7,6},{8,9},{9,8},{10,11... | collective-permute-start | bytes 236204 | tf_op jit(solution)/shard_map/ppermute | solution.py:700
  13.5 4.6 %collective-permute-start.1 = (f32[2,2,32,128]{3,2,0,1:T(8,128)S(1)}, f32[2,2,32,128]{3,2,0,1:T(8,128)S(1)}, u32[]{:S(2)}, u32[]{:S(2)}) collective-permute-start(f32[2,2,32,128]{3,2,0,1:T(8,128)S(1)} %get-tuple-element.32), channel_id=1, source_target_pairs={{0,8},{4,12},{8,0},{12,4},{16,24},{20,28},{24,16},{28,20},{1,9},{5... | collective-permute-start | bytes 196616 | tf_op jit(solution)/shard_map/ppermute | solution.py:700
  15.3 6.4 %collective-permute-start.4 = (f32[2,27,1,729]{3,2,1,0:T(1,128)S(1)}, f32[2,27,1,729]{3,2,1,0:T(1,128)S(1)}, u32[]{:S(2)}, u32[]{:S(2)}) collective-permute-start(f32[2,27,1,729]{3,2,1,0:T(1,128)S(1)} %pad_maximum_fusion), channel_id=1, source_target_pairs={{0,2},{1,3},{2,0},{3,1},{4,6},{5,7},{6,4},{7,5},{8,10},{9,11},{10,... | collective-permute-start | bytes 472400 | tf_op jit(solution)/shard_map/ppermute | solution.py:700
  18.1 6.3 %collective-permute-start.2 = (f32[4,1,32,128]{3,2,0,1:T(8,128)S(1)}, f32[4,1,32,128]{3,2,0,1:T(8,128)S(1)}, u32[]{:S(2)}, u32[]{:S(2)}) collective-permute-start(f32[4,1,32,128]{3,2,0,1:T(8,128)S(1)} %get-tuple-element.35), channel_id=1, source_target_pairs={{0,4},{4,0},{8,12},{12,8},{16,20},{20,16},{24,28},{28,24},{1,5},{5... | collective-permute-start | bytes 196616 | tf_op jit(solution)/shard_map/ppermute | solution.py:700

commit v4 on v3

--- a/solution.py
+++ b/solution.py
@@ -321,9 +321,9 @@
     out_ref[...] = element_pairs(
         groups,
         ahead,
-        (outer_ref[0], outer_ref[1]),
-        (inner_ref[0], inner_ref[1]),
-        (((0,),), ((1,), (2,))),
+        (outer_ref[0], outer_ref[1], outer_ref[1]),
+        (inner_ref[0], inner_ref[1], inner_ref[1]),
+        (((0,),), ((1,),), ((2,),)),
         back_ref[...],
         weight_ref,
         0,
@@ -581,7 +581,7 @@
         mid_l,
         prod,
         heads,
-        {0: start, 1: go_on, 2: end},
+        {1: start, 2: go_on, 3: end},
     )
     is_pressure = lax.axis_index("sub") == FIELDS - 1
     factor = jnp.where(is_pressure, -stabilize, 1.0).astype(f32)

time: 27.6 us -> 27.2 us (0.986)
  Pallas kernels: 14.3 us -> 13.9 us
where the time goes in v4:
time: 27.2 us; the launch traced here: 27 us
  Pallas kernels  13.9 us (51%)
  starting transfers between devices  8.91 us (33%)
  waiting for transfers between devices  3.3 us (12%)
  between operations  0.71 us (3%)
    ppermute x5, starting transfers between devices, swap(): return lax.ppermute(array, axis, [(n, n ^ mask) for n in range(size)])  8.91 us
    pallas_call x2, Pallas kernels, stiff_call(): pl.pallas_call(functools.partial(stiff_kernel, groups, lanes), out_shape=...  6 us
    ppermute x5, waiting for transfers between devices, swap(): return lax.ppermute(array, axis, [(n, n ^ mask) for n in range(size)])  3.3 us
    pallas_call x1, Pallas kernels, final_call(): pl.pallas_call(functools.partial(final_kernel, groups), out_shape=(jax.Sh...  2.84 us
    pallas_call x1, Pallas kernels, volume_call(): pl.pallas_call(functools.partial(volume_kernel, groups), out_shape=(jax.S...  2.63 us
    pallas_call x1, Pallas kernels, prep_call(): pl.pallas_call(functools.partial(prep_kernel, masks), out_shape=(jax.Shap...  2.47 us
  transfers between devices with their start and end apart: 5, of which 2 were waited for; matrix products, arithmetic and copies ran while one was open for 1% of the time, Pallas kernels for 32%

profile of v4, /device:TPU:0, one launch (start us, length us, event | category | flops | bytes accessed | tf_op | source)
XLA Modules:
  0.0 27.0 jit_solution(17419296898768819982)
XLA Ops:
  0.6 0.0 copy-start
  0.6 2.5 %shard_map.122 = (f32[8,32,128]{2,1,0:T(8,128)S(1)}, f32[32,896]{1,0:T(8,128)S(1)}, f32[8,2,32,32]{3,2,1,0:T(8,128)S(1)}, s32[1,128]{1,0:T(1,128)S(1)}, bf16[3,2...) custom-call(s32[6,32]{1,0:T(8,128)} %bitcast.19, ...), custom_call_target="tpu_custom_call" | custom-call | tf_op jit(solution)/shard_map/pallas_call | solution.py:655
  3.1 4.1 %collective-permute-start = (f32[1,4,32,128]{3,2,0,1:T(8,128)S(1)}, f32[1,4,32,128]{3,2,0,1:T(8,128)S(1)}, u32[]{:S(2)}, u32[]{:S(2)}) collective-permute-start(f32[1,4,32,128]{3,2,0,1:T(8,128)S(1)} %get-tuple-element.48), channel_id=1, source_target_pairs={{0,16},{4,20},{8,24},{12,28},{16,0},{20,4},{24,8},{28,12},{1,17},{... | collective-permute-start | bytes 196616 | tf_op jit(solution)/shard_map/ppermute | solution.py:700
  7.3 0.0 copy-done
  7.3 0.0 collective-permute-start.3
  7.3 3.0 %shard_map.123 = (f32[32,896]{1,0:T(8,128)S(1)}, f32[96,4608]{1,0:T(8,128)S(1)}) custom-call(f32[32,896]{1,0:T(8,128)S(1)} %get-tuple-element.25.wide_ref, bf16[384,1152]{1,0:T(8,128)(2,1)S(1)} %get-tuple-element.26.ahead_ref, bf16[2,96,96]{2,1,0:T(8,128)(2,1)S(1)} %get-tuple-element.27.outer_ref, bf16[2,64,192]{2,1,0:T(8,128)(2,1)S(1)} %get-tuple-element.28.inner_ref, ...), custom_call_target="tpu_custom_call" | custom-call | tf_op jit(solution)/shard_map/pallas_call | solution.py:613
  10.3 3.0 %shard_map.124 = (f32[32,896]{1,0:T(8,128)S(1)}, f32[96,9216]{1,0:T(8,128)S(1)}) custom-call(f32[32,896]{1,0:T(8,128)S(1)} %get-tuple-element.25.wide_ref, bf16[384,1152]{1,0:T(8,128)(2,1)S(1)} %get-tuple-element.26.ahead_ref, bf16[2,96,96]{2,1,0:T(8,128)(2,1)S(1)} %get-tuple-element.27.outer_ref, bf16[2,64,192]{2,1,0:T(8,128)(2,1)S(1)} %get-tuple-element.28.inner_ref, ...), custom_call_target="tpu_custom_call" | custom-call | tf_op jit(solution)/shard_map/pallas_call | solution.py:613
  13.3 0.0 collective-permute-done
  13.3 1.6 %collective-permute-start.1 = (f32[2,2,32,128]{3,2,0,1:T(8,128)S(1)}, f32[2,2,32,128]{3,2,0,1:T(8,128)S(1)}, u32[]{:S(2)}, u32[]{:S(2)}) collective-permute-start(f32[2,2,32,128]{3,2,0,1:T(8,128)S(1)} %get-tuple-element.32), channel_id=1, source_target_pairs={{0,8},{4,12},{8,0},{12,4},{16,24},{20,28},{24,16},{28,20},{1,9},{5... | collective-permute-start | bytes 196616 | tf_op jit(solution)/shard_map/ppermute | solution.py:700
  15.0 0.0 collective-permute-done.3.near_ref
  15.0 0.1 pad_maximum_fusion
  15.1 1.6 %collective-permute-start.4 = (f32[2,27,1,729]{3,2,1,0:T(1,128)S(1)}, f32[2,27,1,729]{3,2,1,0:T(1,128)S(1)}, u32[]{:S(2)}, u32[]{:S(2)}) collective-permute-start(f32[2,27,1,729]{3,2,1,0:T(1,128)S(1)} %pad_maximum_fusion), channel_id=1, source_target_pairs={{0,2},{1,3},{2,0},{3,1},{4,6},{5,7},{6,4},{7,5},{8,10},{9,11},{10,... | collective-permute-start | bytes 472400 | tf_op jit(solution)/shard_map/ppermute | solution.py:700
  16.7 1.2 %collective-permute-done.1 = f32[2,2,32,128]{3,2,0,1:T(8,128)S(1)} collective-permute-done((f32[2,2,32,128]{3,2,0,1:T(8,128)S(1)}, f32[2,2,32,128]{3,2,0,1:T(8,128)S(1)}, u32[]{:S(2)}, u32[]{:S(2)}) %collective-permute-start.1) | collective-permute-done | bytes 65568 | tf_op jit(solution)/shard_map/ppermute | solution.py:700
  17.9 1.6 %collective-permute-start.2 = (f32[4,1,32,128]{3,2,0,1:T(8,128)S(1)}, f32[4,1,32,128]{3,2,0,1:T(8,128)S(1)}, u32[]{:S(2)}, u32[]{:S(2)}) collective-permute-start(f32[4,1,32,128]{3,2,0,1:T(8,128)S(1)} %get-tuple-element.35), channel_id=1, source_target_pairs={{0,4},{4,0},{8,12},{12,8},{16,20},{20,16},{24,28},{28,24},{1,5},{5... | collective-permute-start | bytes 196616 | tf_op jit(solution)/shard_map/ppermute | solution.py:700
  19.5 2.1 %collective-permute-done.4.far_ref = f32[2,27,1,729]{3,2,1,0:T(1,128)S(1)} collective-permute-done((f32[2,27,1,729]{3,2,1,0:T(1,128)S(1)}, f32[2,27,1,729]{3,2,1,0:T(1,128)S(1)}, u32[]{:S(2)}, u32[]{:S(2)}) %collective-permute-start.4) | collective-permute-done | bytes 157496 | tf_op jit(solution)/shard_map/ppermute | solution.py:700
  21.6 2.6 %shard_map.125 = (f32[32,896]{1,0:T(8,128)S(1)}, f32[3,32,896]{2,1,0:T(8,128)S(1)}) custom-call(f32[27,1,729]{2,1,0:T(1,128)S(1)} %collective-permute-done.3.near_ref, f32[2,27,1,729]{3,2,1,0:T(1,128)S(1)} %collective-permute-done.4.far_ref, bf16[3,256,384]{2,1,0:T(8,128)(2,1)S(1)} %get-tuple-element.36.spread_ref, ...), custom_call_target="tpu_custom_call" | custom-call | tf_op jit(solution)/shard_map/pallas_call | solution.py:642
  24.2 0.0 collective-permute-done.2
  24.2 2.8 %shard_map.126 = (f32[27,1,729]{2,1,0:T(1,128)}, f32[4,1,1,729]{3,2,1,0:T(1,128)}) custom-call(s32[1,128]{1,0:T(1,128)S(1)} %get-tuple-element.22.route_vmem, f32[8,2,32,32]{3,2,1,0:T(8,128)S(1)} %get-tuple-element.23.sides_ref, f32[4,32,128]{2,1,0:T(8,128)S(1)} %get-tuple-element.45.kept_ref, f32[4,32,128]{2,1,0:T(8,128)S(1)} %bitcast.14, ...), custom_call_target="tpu_custom_call" | custom-call | tf_op jit(solution)/shard_map/pallas_call | solution.py:683
  (3 shorter events, 0.0 us)
Async XLA Ops:
  0.6 6.6 %copy-start = (f32[1,1,1,27,729]{4,2,3,1,0:T(1,128)S(1)}, f32[1,1,1,27,729]{4,2,3,1,0:T(1,128)}, u32[]{:S(2)}) copy-start(f32[1,1,1,27,729]{4,2,3,1,0:T(1,128)} %param.11) | copy-start | bytes 236200
  3.1 10.2 %collective-permute-start = (f32[1,4,32,128]{3,2,0,1:T(8,128)S(1)}, f32[1,4,32,128]{3,2,0,1:T(8,128)S(1)}, u32[]{:S(2)}, u32[]{:S(2)}) collective-permute-start(f32[1,4,32,128]{3,2,0,1:T(8,128)S(1)} %get-tuple-element.48), channel_id=1, source_target_pairs={{0,16},{4,20},{8,24},{12,28},{16,0},{20,4},{24,8},{28,12},{1,17},{... | collective-permute-start | bytes 196616 | tf_op jit(solution)/shard_map/ppermute | solution.py:700
  7.3 7.7 %collective-permute-start.3 = (f32[27,1,729]{2,1,0:T(1,128)S(1)}, f32[27,1,729]{2,1,0:T(1,128)S(1)}, u32[]{:S(2)}, u32[]{:S(2)}) collective-permute-start(f32[27,1,729]{2,1,0:T(1,128)S(1)} %bitcast.16), channel_id=1, source_target_pairs={{0,1},{1,0},{2,3},{3,2},{4,5},{5,4},{6,7},{7,6},{8,9},{9,8},{10,11... | collective-permute-start | bytes 236204 | tf_op jit(solution)/shard_map/ppermute | solution.py:700
  13.3 4.6 %collective-permute-start.1 = (f32[2,2,32,128]{3,2,0,1:T(8,128)S(1)}, f32[2,2,32,128]{3,2,0,1:T(8,128)S(1)}, u32[]{:S(2)}, u32[]{:S(2)}) collective-permute-start(f32[2,2,32,128]{3,2,0,1:T(8,128)S(1)} %get-tuple-element.32), channel_id=1, source_target_pairs={{0,8},{4,12},{8,0},{12,4},{16,24},{20,28},{24,16},{28,20},{1,9},{5... | collective-permute-start | bytes 196616 | tf_op jit(solution)/shard_map/ppermute | solution.py:700
  15.1 6.5 %collective-permute-start.4 = (f32[2,27,1,729]{3,2,1,0:T(1,128)S(1)}, f32[2,27,1,729]{3,2,1,0:T(1,128)S(1)}, u32[]{:S(2)}, u32[]{:S(2)}) collective-permute-start(f32[2,27,1,729]{3,2,1,0:T(1,128)S(1)} %pad_maximum_fusion), channel_id=1, source_target_pairs={{0,2},{1,3},{2,0},{3,1},{4,6},{5,7},{6,4},{7,5},{8,10},{9,11},{10,... | collective-permute-start | bytes 472400 | tf_op jit(solution)/shard_map/ppermute | solution.py:700
  17.9 6.3 %collective-permute-start.2 = (f32[4,1,32,128]{3,2,0,1:T(8,128)S(1)}, f32[4,1,32,128]{3,2,0,1:T(8,128)S(1)}, u32[]{:S(2)}, u32[]{:S(2)}) collective-permute-start(f32[4,1,32,128]{3,2,0,1:T(8,128)S(1)} %get-tuple-element.35), channel_id=1, source_target_pairs={{0,4},{4,0},{8,12},{12,8},{16,20},{20,16},{24,28},{28,24},{1,5},{5... | collective-permute-start | bytes 196616 | tf_op jit(solution)/shard_map/ppermute | solution.py:700

commit v5 on v4

--- a/solution.py
+++ b/solution.py
@@ -23,6 +23,7 @@
 EARLY = GROUPS - 2
 WIDE = (GROUPS + 1) * WIN
 FLAT = 768
+LAST = (BASIS - 1) * BASIS - (FLAT - WIN)
 GROUP_ROWS = 4 * PAD
 BLOCK = 256
 BLOCK_WIDE = 384
@@ -231,8 +232,12 @@
 def gather_back(heads_ref, n, back):
     high = heads_ref[n * GROUP_ROWS : (n + 1) * GROUP_ROWS, :]
     low = heads_ref[heads_ref.shape[0] // 2 + n * GROUP_ROWS : heads_ref.shape[0] // 2 + (n + 1) * GROUP_ROWS, :]
-    out = dot(jnp.concatenate([high, low], axis=0), back)
-    out = out[:GROUP_ROWS] + out[GROUP_ROWS:]
+    if back.shape[0] == SPAN:
+        lower = jnp.concatenate([back[:, :WIN], jnp.zeros((SPAN, WIN), bf16)], axis=1)
+        out = dot(jnp.concatenate([high, low], axis=1), jnp.concatenate([back, lower], axis=0))
+    else:
+        out = dot(jnp.concatenate([high, low], axis=0), back)
+        out = out[:GROUP_ROWS] + out[GROUP_ROWS:]
     return out[:, :WIN] + out[:, WIN:]
 
 
@@ -484,25 +489,24 @@
     for s in range(slots):
         line[s : s + 1, : BASIS * BASIS] = lag[s, 0]
     spreads = [jnp.where(same, line[s : s + 1, :], 0.0) for s in range(slots)]
-    spreads += [
-        jnp.where(same, flat[0:1, :], 0.0),
-        jnp.where(same, flat[BASIS - 1 : BASIS, :], 0.0),
-        jnp.where(group == 0, flat[...], 0.0),
-        jnp.where(group == BASIS - 1, flat[...], 0.0),
-    ]
+    spreads += [jnp.where(same, flat[0:1, :], 0.0), jnp.where(same, flat[BASIS - 1 : BASIS, :], 0.0)]
     parts = []
     for x in spreads:
         parts.extend(split(x))
-    squares = halves_sum(dot_nt(jnp.concatenate(parts, axis=0), fold), 4 + slots)
+    squares = dot_nt(jnp.concatenate(parts, axis=0), fold)
+    copies[5].wait()
+    (wide,) = expand([flat[...]], spread_ref)
+    wide_ref[...] = wide
+    squares = halves_sum(squares, 2 + slots)
+    inside = lax.broadcasted_iota(jnp.int32, (PAD, PAD), 1) < BASIS
+    last = pltpu.roll(flat[:, FLAT - WIN :], WIN - LAST, axis=1)
+    squares += [jnp.where(inside, flat[:, :PAD], 0.0), jnp.where(inside, last[:, :PAD], 0.0)]
     base = mine * slots
     for s in range(slots):
         for side in range(2):
             for d in range(2):
                 sides_ref[2 * s + side, d, :BASIS, :BASIS] = masked(mortar[s, side, :, d, :], links[4 + d, base + s])
     halfway = [dot_split(sides_ref[t, 0], squares[t // 2], ((0,), (0,))) for t in range(items)]
-    copies[5].wait()
-    (wide,) = expand([flat[...]], spread_ref)
-    wide_ref[...] = wide
     for f in range(4):
         patch, first, second = faces[f]
         row = jnp.bitwise_xor(mine, patch)
@@ -552,22 +556,24 @@
         both.extend(dot_split(halfway[t], sides_ref[t, 1], ((1,), (1,))) for t in range(items))
 
     def end():
+        parts = []
+        for x in squares[:2] + [both[2 * s] - both[2 * s + 1] for s in range(slots)]:
+            parts.extend(split(x))
+        lines = halves_sum(dot(jnp.concatenate(parts, axis=0), fold), 2 + slots)
         for s in range(slots):
-            squares.append(both[2 * s] - both[2 * s + 1])
-        parts = []
-        for x in squares:
-            parts.extend(split(x))
-        lines = halves_sum(dot(jnp.concatenate(parts, axis=0), fold), 4 + slots)
-        for s in range(slots):
-            row = jnp.sum(jnp.where(same, lines[4 + s], 0.0), axis=0, keepdims=True)
+            row = jnp.sum(jnp.where(same, lines[2 + s], 0.0), axis=0, keepdims=True)
             jump_ref[s, 0] = row[:, : BASIS * BASIS]
         low_row = jnp.sum(jnp.where(same, lines[0], 0.0), axis=0, keepdims=True)
         high_row = jnp.sum(jnp.where(same, lines[1], 0.0), axis=0, keepdims=True)
+        low_layer = jnp.concatenate([squares[2], jnp.zeros((PAD, FLAT - PAD), f32)], axis=1)
+        high_layer = jnp.concatenate([squares[3], jnp.zeros((PAD, WIN - PAD), f32)], axis=1)
+        high_layer = jnp.concatenate(
+            [jnp.zeros((PAD, FLAT - WIN), f32), pltpu.roll(high_layer, LAST, axis=1)], axis=1
+        )
         both.append(
             jnp.where(rows == 0, low_row, 0.0)
             + jnp.where(rows == BASIS - 1, high_row, 0.0)
-            + jnp.where(group == 0, lines[2], 0.0)
-            + jnp.where(group == BASIS - 1, lines[3], 0.0)
+            + (low_layer + high_layer)
         )
 
     tables = volume_tables(outer_ref, inner_ref, back_ref)

time: 27.2 us -> 27 us (level)
  no operation moved by 1% of the time
where the time goes in v5:
time: 27 us; the launch traced here: 26.9 us
  Pallas kernels  13.7 us (51%)
  starting transfers between devices  8.91 us (33%)
  waiting for transfers between devices  3.3 us (12%)
  between operations  0.71 us (3%)
    ppermute x5, starting transfers between devices, swap(): return lax.ppermute(array, axis, [(n, n ^ mask) for n in range(size)])  8.91 us
    pallas_call x2, Pallas kernels, stiff_call(): pl.pallas_call(functools.partial(stiff_kernel, groups, lanes), out_shape=...  6 us
    ppermute x5, waiting for transfers between devices, swap(): return lax.ppermute(array, axis, [(n, n ^ mask) for n in range(size)])  3.3 us
    pallas_call x1, Pallas kernels, final_call(): pl.pallas_call(functools.partial(final_kernel, groups), out_shape=(jax.Sh...  2.77 us
    pallas_call x1, Pallas kernels, volume_call(): pl.pallas_call(functools.partial(volume_kernel, groups), out_shape=(jax.S...  2.5 us
    pallas_call x1, Pallas kernels, prep_call(): pl.pallas_call(functools.partial(prep_kernel, masks), out_shape=(jax.Shap...  2.47 us
  transfers between devices with their start and end apart: 5, of which 2 were waited for; matrix products, arithmetic and copies ran while one was open for 1% of the time, Pallas kernels for 32%

profile of v5, /device:TPU:0, one launch (start us, length us, event | category | flops | bytes accessed | tf_op | source)
XLA Modules:
  0.0 26.9 jit_solution(4534390416439973483)
XLA Ops:
  0.6 0.0 copy-start
  0.6 2.5 %shard_map.122 = (f32[8,32,128]{2,1,0:T(8,128)S(1)}, f32[32,896]{1,0:T(8,128)S(1)}, f32[8,2,32,32]{3,2,1,0:T(8,128)S(1)}, s32[1,128]{1,0:T(1,128)S(1)}, bf16[3,2...) custom-call(s32[6,32]{1,0:T(8,128)} %bitcast.19, ...), custom_call_target="tpu_custom_call" | custom-call | tf_op jit(solution)/shard_map/pallas_call | solution.py:661
  3.1 4.1 %collective-permute-start = (f32[1,4,32,128]{3,2,0,1:T(8,128)S(1)}, f32[1,4,32,128]{3,2,0,1:T(8,128)S(1)}, u32[]{:S(2)}, u32[]{:S(2)}) collective-permute-start(f32[1,4,32,128]{3,2,0,1:T(8,128)S(1)} %get-tuple-element.48), channel_id=1, source_target_pairs={{0,16},{4,20},{8,24},{12,28},{16,0},{20,4},{24,8},{28,12},{1,17},{... | collective-permute-start | bytes 196616 | tf_op jit(solution)/shard_map/ppermute | solution.py:706
  7.3 0.0 copy-done
  7.3 0.0 collective-permute-start.3
  7.3 3.0 %shard_map.123 = (f32[32,896]{1,0:T(8,128)S(1)}, f32[96,4608]{1,0:T(8,128)S(1)}) custom-call(f32[32,896]{1,0:T(8,128)S(1)} %get-tuple-element.25.wide_ref, bf16[384,1152]{1,0:T(8,128)(2,1)S(1)} %get-tuple-element.26.ahead_ref, bf16[2,96,96]{2,1,0:T(8,128)(2,1)S(1)} %get-tuple-element.27.outer_ref, bf16[2,64,192]{2,1,0:T(8,128)(2,1)S(1)} %get-tuple-element.28.inner_ref, ...), custom_call_target="tpu_custom_call" | custom-call | tf_op jit(solution)/shard_map/pallas_call | solution.py:619
  10.3 3.0 %shard_map.124 = (f32[32,896]{1,0:T(8,128)S(1)}, f32[96,9216]{1,0:T(8,128)S(1)}) custom-call(f32[32,896]{1,0:T(8,128)S(1)} %get-tuple-element.25.wide_ref, bf16[384,1152]{1,0:T(8,128)(2,1)S(1)} %get-tuple-element.26.ahead_ref, bf16[2,96,96]{2,1,0:T(8,128)(2,1)S(1)} %get-tuple-element.27.outer_ref, bf16[2,64,192]{2,1,0:T(8,128)(2,1)S(1)} %get-tuple-element.28.inner_ref, ...), custom_call_target="tpu_custom_call" | custom-call | tf_op jit(solution)/shard_map/pallas_call | solution.py:619
  13.3 0.0 collective-permute-done
  13.3 1.6 %collective-permute-start.1 = (f32[2,2,32,128]{3,2,0,1:T(8,128)S(1)}, f32[2,2,32,128]{3,2,0,1:T(8,128)S(1)}, u32[]{:S(2)}, u32[]{:S(2)}) collective-permute-start(f32[2,2,32,128]{3,2,0,1:T(8,128)S(1)} %get-tuple-element.32), channel_id=1, source_target_pairs={{0,8},{4,12},{8,0},{12,4},{16,24},{20,28},{24,16},{28,20},{1,9},{5... | collective-permute-start | bytes 196616 | tf_op jit(solution)/shard_map/ppermute | solution.py:706
  15.0 0.0 collective-permute-done.3.near_ref
  15.0 0.1 pad_maximum_fusion
  15.1 1.6 %collective-permute-start.4 = (f32[2,27,1,729]{3,2,1,0:T(1,128)S(1)}, f32[2,27,1,729]{3,2,1,0:T(1,128)S(1)}, u32[]{:S(2)}, u32[]{:S(2)}) collective-permute-start(f32[2,27,1,729]{3,2,1,0:T(1,128)S(1)} %pad_maximum_fusion), channel_id=1, source_target_pairs={{0,2},{1,3},{2,0},{3,1},{4,6},{5,7},{6,4},{7,5},{8,10},{9,11},{10,... | collective-permute-start | bytes 472400 | tf_op jit(solution)/shard_map/ppermute | solution.py:706
  16.7 1.2 %collective-permute-done.1 = f32[2,2,32,128]{3,2,0,1:T(8,128)S(1)} collective-permute-done((f32[2,2,32,128]{3,2,0,1:T(8,128)S(1)}, f32[2,2,32,128]{3,2,0,1:T(8,128)S(1)}, u32[]{:S(2)}, u32[]{:S(2)}) %collective-permute-start.1) | collective-permute-done | bytes 65568 | tf_op jit(solution)/shard_map/ppermute | solution.py:706
  17.9 1.6 %collective-permute-start.2 = (f32[4,1,32,128]{3,2,0,1:T(8,128)S(1)}, f32[4,1,32,128]{3,2,0,1:T(8,128)S(1)}, u32[]{:S(2)}, u32[]{:S(2)}) collective-permute-start(f32[4,1,32,128]{3,2,0,1:T(8,128)S(1)} %get-tuple-element.35), channel_id=1, source_target_pairs={{0,4},{4,0},{8,12},{12,8},{16,20},{20,16},{24,28},{28,24},{1,5},{5... | collective-permute-start | bytes 196616 | tf_op jit(solution)/shard_map/ppermute | solution.py:706
  19.5 2.1 %collective-permute-done.4.far_ref = f32[2,27,1,729]{3,2,1,0:T(1,128)S(1)} collective-permute-done((f32[2,27,1,729]{3,2,1,0:T(1,128)S(1)}, f32[2,27,1,729]{3,2,1,0:T(1,128)S(1)}, u32[]{:S(2)}, u32[]{:S(2)}) %collective-permute-start.4) | collective-permute-done | bytes 157496 | tf_op jit(solution)/shard_map/ppermute | solution.py:706
  21.6 2.5 %shard_map.125 = (f32[32,896]{1,0:T(8,128)S(1)}, f32[3,32,896]{2,1,0:T(8,128)S(1)}) custom-call(f32[27,1,729]{2,1,0:T(1,128)S(1)} %collective-permute-done.3.near_ref, f32[2,27,1,729]{3,2,1,0:T(1,128)S(1)} %collective-permute-done.4.far_ref, bf16[3,256,384]{2,1,0:T(8,128)(2,1)S(1)} %get-tuple-element.36.spread_ref, ...), custom_call_target="tpu_custom_call" | custom-call | tf_op jit(solution)/shard_map/pallas_call | solution.py:648
  24.1 0.0 collective-permute-done.2
  24.1 2.8 %shard_map.126 = (f32[27,1,729]{2,1,0:T(1,128)}, f32[4,1,1,729]{3,2,1,0:T(1,128)}) custom-call(s32[1,128]{1,0:T(1,128)S(1)} %get-tuple-element.22.route_vmem, f32[8,2,32,32]{3,2,1,0:T(8,128)S(1)} %get-tuple-element.23.sides_ref, f32[4,32,128]{2,1,0:T(8,128)S(1)} %get-tuple-element.45.kept_ref, f32[4,32,128]{2,1,0:T(8,128)S(1)} %bitcast.14, ...), custom_call_target="tpu_custom_call" | custom-call | tf_op jit(solution)/shard_map/pallas_call | solution.py:689
  (3 shorter events, 0.0 us)
Async XLA Ops:
  0.6 6.6 %copy-start = (f32[1,1,1,27,729]{4,2,3,1,0:T(1,128)S(1)}, f32[1,1,1,27,729]{4,2,3,1,0:T(1,128)}, u32[]{:S(2)}) copy-start(f32[1,1,1,27,729]{4,2,3,1,0:T(1,128)} %param.11) | copy-start | bytes 236200
  3.1 10.2 %collective-permute-start = (f32[1,4,32,128]{3,2,0,1:T(8,128)S(1)}, f32[1,4,32,128]{3,2,0,1:T(8,128)S(1)}, u32[]{:S(2)}, u32[]{:S(2)}) collective-permute-start(f32[1,4,32,128]{3,2,0,1:T(8,128)S(1)} %get-tuple-element.48), channel_id=1, source_target_pairs={{0,16},{4,20},{8,24},{12,28},{16,0},{20,4},{24,8},{28,12},{1,17},{... | collective-permute-start | bytes 196616 | tf_op jit(solution)/shard_map/ppermute | solution.py:706
  7.3 7.7 %collective-permute-start.3 = (f32[27,1,729]{2,1,0:T(1,128)S(1)}, f32[27,1,729]{2,1,0:T(1,128)S(1)}, u32[]{:S(2)}, u32[]{:S(2)}) collective-permute-start(f32[27,1,729]{2,1,0:T(1,128)S(1)} %bitcast.16), channel_id=1, source_target_pairs={{0,1},{1,0},{2,3},{3,2},{4,5},{5,4},{6,7},{7,6},{8,9},{9,8},{10,11... | collective-permute-start | bytes 236204 | tf_op jit(solution)/shard_map/ppermute | solution.py:706
  13.3 4.6 %collective-permute-start.1 = (f32[2,2,32,128]{3,2,0,1:T(8,128)S(1)}, f32[2,2,32,128]{3,2,0,1:T(8,128)S(1)}, u32[]{:S(2)}, u32[]{:S(2)}) collective-permute-start(f32[2,2,32,128]{3,2,0,1:T(8,128)S(1)} %get-tuple-element.32), channel_id=1, source_target_pairs={{0,8},{4,12},{8,0},{12,4},{16,24},{20,28},{24,16},{28,20},{1,9},{5... | collective-permute-start | bytes 196616 | tf_op jit(solution)/shard_map/ppermute | solution.py:706
  15.1 6.5 %collective-permute-start.4 = (f32[2,27,1,729]{3,2,1,0:T(1,128)S(1)}, f32[2,27,1,729]{3,2,1,0:T(1,128)S(1)}, u32[]{:S(2)}, u32[]{:S(2)}) collective-permute-start(f32[2,27,1,729]{3,2,1,0:T(1,128)S(1)} %pad_maximum_fusion), channel_id=1, source_target_pairs={{0,2},{1,3},{2,0},{3,1},{4,6},{5,7},{6,4},{7,5},{8,10},{9,11},{10,... | collective-permute-start | bytes 472400 | tf_op jit(solution)/shard_map/ppermute | solution.py:706
  17.9 6.2 %collective-permute-start.2 = (f32[4,1,32,128]{3,2,0,1:T(8,128)S(1)}, f32[4,1,32,128]{3,2,0,1:T(8,128)S(1)}, u32[]{:S(2)}, u32[]{:S(2)}) collective-permute-start(f32[4,1,32,128]{3,2,0,1:T(8,128)S(1)} %get-tuple-element.35), channel_id=1, source_target_pairs={{0,4},{4,0},{8,12},{12,8},{16,20},{20,16},{24,28},{28,24},{1,5},{5... | collective-permute-start | bytes 196616 | tf_op jit(solution)/shard_map/ppermute | solution.py:706
